TPU v7x, 8 devices: a whole 2x2x1 slice. The times are simulated.
8 devices in a mesh: rep: 1 (over z), model: 2 (over y), vocab: 4 (over x, core).
Axes of the slice: x: 2, y: 2, z: 1, core: 2. Of those that a mesh axis runs over, the one named last changes fastest.
Arguments:
- hidden: bfloat16 [256, 5120], P(('rep', 'model', 'vocab'))
- head_rows: bfloat16 [131072, 5120], P(('model', 'vocab'))
- allowed_ids: int32 [256, 64], P(('rep', 'model', 'vocab'))
- valid_mask: int32 [256, 64], P(('rep', 'model', 'vocab'))
- target_pos: int32 [256], P(('rep', 'model', 'vocab'))
Outputs:
- output 1: float32 [256, 64], P(('rep', 'model', 'vocab'))
- output 2: float32 [256], P(('rep', 'model', 'vocab'))
All inputs are finite; a program needn't handle non-finite values.
Results may differ from a plain program's by a relative error of at most 0.001.
Values are sent between devices in bfloat16 or wider.
A program may use at most 1 GiB of HBM per device.

v0:
```python
import jax
import jax.numpy as jnp
from jax import lax
from jax.sharding import PartitionSpec as P

value_a11 = 0.5
OWNER_SHARE = 4


def masked_softmax(scores, is_valid, target_pos):
    scores = jnp.where(is_valid, scores, -jnp.inf)
    top_score = jnp.max(scores, axis=1, keepdims=True)
    log_norm = top_score[:, 0] + jnp.log(jnp.sum(jnp.exp(scores - top_score), axis=1))
    probs = jnp.where(is_valid, jnp.exp(scores - log_norm[:, None]), 0.0)
    picked_score = jnp.take_along_axis(scores, target_pos[:, None], axis=1)[:, 0]
    return probs, picked_score - log_norm


def solution(mesh):
    shard_axes = ('model', 'vocab')
    num_shards = mesh.shape['model'] * mesh.shape['vocab']
    row_spec = P(('rep', 'model', 'vocab'), None)
    vec_spec = P(('rep', 'model', 'vocab'))

    def local_step(hidden, head_rows, allowed_ids, valid_mask, target_pos):
        rows_loc, list_len = allowed_ids.shape
        shard_len = head_rows.shape[0]
        row_cap = list_len // OWNER_SHARE
        is_valid = valid_mask > 0
        shard_of = allowed_ids // shard_len
        offset = allowed_ids - shard_of * shard_len
        owner_shard = jnp.where(is_valid, shard_of, num_shards)
        own_hits = (owner_shard[:, :, None] == jnp.arange(num_shards, dtype=jnp.int32)).astype(jnp.int32)
        slot_rank = jnp.maximum(jnp.sum(jnp.cumsum(own_hits, axis=1) * own_hits, axis=2) - 1, 0)
        row_idx = jnp.arange(rows_loc, dtype=jnp.int32)[:, None]
        send_ids = jnp.zeros((num_shards, rows_loc, row_cap), jnp.int32)
        send_ids = send_ids.at[owner_shard, row_idx, slot_rank].set(offset, mode='drop')
        hidden_all = lax.all_gather(hidden, shard_axes)
        recv_ids = lax.all_to_all(send_ids, shard_axes, 0, 0)
        picked = head_rows[recv_ids]
        part_scores = jnp.einsum('sbcd,sbd->sbc', picked, hidden_all, preferred_element_type=jnp.float32)
        back_scores = lax.all_to_all(part_scores, shard_axes, 0, 0)
        safe_owner = jnp.minimum(owner_shard, num_shards - 1)
        scores = back_scores[safe_owner, row_idx, slot_rank] / value_a11
        return masked_softmax(scores, is_valid, target_pos)

    program = jax.shard_map(local_step, mesh=mesh, in_specs=(row_spec, P(shard_axes, None), row_spec, row_spec, vec_spec), out_specs=(row_spec, vec_spec), check_vma=False)
    return program
```

profile of v0, /device:TPU:0, one launch (start us, length us, event | category | flops | bytes accessed | tf_op | source)
XLA Modules:
  0.0 421.8 jit_solution(7695836181153636409)
XLA Ops:
  7.2 0.0 all-gather.3.cloned.1.call-start
  7.2 0.7 all-gather.3.cloned.1.call-update
  7.9 0.8 fusion.6
  8.7 0.1 reshape.79
  8.7 0.1 copy.15
  8.8 1.7 select_reduce_fusion
  10.5 0.1 copy.16
  10.6 0.7 multiply_reduce_fusion
  11.4 0.7 and_reduce_fusion
  12.1 0.1 reshape.77
  12.2 8.1 %scatter_custom_fusion = s32[4096]{0:T(1024)S(1)} fusion(s32[2048]{0:T(1024)S(1)} %reshape.77, s32[2048]{0:T(1024)S(1)} %reshape.79, s32[]{:T(128)} %constant.24.clone.1), kind=kCustom, calls=%fused_computation.36 | custom fusion | bytes 16388
  20.2 0.1 reshape.53
  20.3 0.7 reshape.98
  21.0 4.3 %all-to-all-start = ((s32[8,1,512]{2,1,0:T(1,128)}), s32[8,1,512]{2,1,0:T(1,128)S(1)}, u32[]{:S(2)}, u32[]{:S(2)}) async-start(s32[8,1,512]{2,1,0:T(1,128)} %reshape.98), calls=%async_computation | async-start | bytes 32768 | tf_op jit(solution)/shard_map/all_to_all | solution.py:39
  25.3 0.7 fusion.17
  26.0 4.0 all-to-all-done
  30.1 0.5 broadcast.160
  30.6 0.7 reduce.4
  31.3 0.1 reshape.99
  31.4 0.1 copy.17
  31.5 0.1 reshape.57
  31.6 152.4 %gather_fusion = bf16[4096,5120]{1,0:T(8,128)(2,1)} fusion(bf16[16384,5120]{1,0:T(8,128)(2,1)} %param.6, s32[4096]{0:T(1024)S(1)} %broadcast_clamp_fusion), kind=kCustom, calls=%fused_computation | custom fusion | bytes 83902464 | tf_op jit(solution)/shard_map/gather | solution.py:40
  184.0 0.0 all-gather.3.cloned.1.call-done
  184.0 0.0 copy-start
  184.0 19.4 %fusion = f32[8,32,1,16]{3,2,1,0:T(1,128)S(1)} fusion(bf16[8,32,16,5120]{3,2,1,0:T(8,128)(2,1)} %bitcast.38, bf16[8,32,5120,1]{2,1,0,3:T(8,128)(2,1)} %bitcast.39), kind=kOutput, calls=%fused_computation.4 | convolution fusion | flops 41943040 | bytes 44580864 | tf_op jit(solution)/shard_map/sbcd,sbd->sbc/dot_general | solution.py:41
  203.4 0.1 copy.19
  203.5 0.7 reshape.100
  204.2 185.2 %all-to-all-start.1 = ((f32[8,1,512]{2,1,0:T(1,128)}), f32[8,1,512]{2,1,0:T(1,128)S(1)}, u32[]{:S(2)}, u32[]{:S(2)}) async-start(f32[8,1,512]{2,1,0:T(1,128)} %reshape.100), calls=%async_computation.1 | async-start | bytes 32768 | tf_op jit(solution)/shard_map/all_to_all | solution.py:42
  389.4 0.1 reshape.63
  389.5 4.5 %all-to-all-done.1 = f32[8,1,512]{2,1,0:T(1,128)S(1)} async-done(((f32[8,1,512]{2,1,0:T(1,128)}), f32[8,1,512]{2,1,0:T(1,128)S(1)}, u32[]{:S(2)}, u32[]{:S(2)}) %all-to-all-start.1) | async-done | bytes 16416 | tf_op jit(solution)/shard_map/all_to_all | solution.py:42
  393.9 0.5 broadcast.161
  394.4 0.7 reduce.5
  395.1 0.1 reshape.101
  395.2 17.5 %gather_fusion.1 = f32[2048]{0:T(1024)S(1)} fusion(f32[8,32,16]{1,2,0:T(8,128)S(1)} %bitcast.37, s32[2048]{0:T(1024)S(1)} %reshape.63), kind=kCustom, calls=%fused_computation.1 | custom fusion | bytes 40960 | tf_op jit(solution)/shard_map/gather | solution.py:44
  412.7 0.1 reshape.88
  412.7 0.1 fusion.18
  412.9 0.7 gather_fusion.2
  413.6 0.2 exponential_reduce_fusion
  413.8 0.0 copy-done
  413.8 0.5 fusion.16
  414.3 0.7 exponential_select_fusion
  (12 shorter events, 0.1 us)
Async XLA Ops:
  7.2 176.8 %all-gather.3.cloned.1.call-start = ((), (), s32[]{:S(2)}) async-start(), calls=%async_computation.2 | async-start | bytes 2949120 | tf_op jit(solution)/shard_map/all_gather | solution.py:38
  21.0 9.0 %all-to-all-start = ((s32[8,1,512]{2,1,0:T(1,128)}), s32[8,1,512]{2,1,0:T(1,128)S(1)}, u32[]{:S(2)}, u32[]{:S(2)}) async-start(s32[8,1,512]{2,1,0:T(1,128)} %reshape.98), calls=%async_computation | async-start | bytes 32768 | tf_op jit(solution)/shard_map/all_to_all | solution.py:39
  184.0 229.8 %copy-start = (s32[32]{0:T(128)S(1)}, s32[32]{0:T(128)}, u32[]{:S(2)}) copy-start(s32[32]{0:T(128)} %param.9) | copy-start | bytes 388
  204.2 189.7 %all-to-all-start.1 = ((f32[8,1,512]{2,1,0:T(1,128)}), f32[8,1,512]{2,1,0:T(1,128)S(1)}, u32[]{:S(2)}, u32[]{:S(2)}) async-start(f32[8,1,512]{2,1,0:T(1,128)} %reshape.100), calls=%async_computation.1 | async-start | bytes 32768 | tf_op jit(solution)/shard_map/all_to_all | solution.py:42
Sparse Core Ops, SparseCore 0:
  9.8 27.1 all-gather.2
where the time goes:
time: 429 us; the launch traced here: 422 us
  starting transfers between devices  190 us (44%)
  local copies, waits for them, and re-layouts  182 us (42%)
  matrix products  19.4 us (5%)
  between operations  14.2 us (3%)
  waiting for transfers between devices  9.16 us (2%)
  other arithmetic  7.54 us (2%)
    all_to_all x1, starting transfers between devices, local_step(): back_scores = lax.all_to_all(part_scores, shard_axes, 0, 0)  185 us
    gather x1, local copies, waits for them, and re-layouts, local_step(): picked = head_rows[recv_ids]  152 us
    dot_general x1, matrix products, local_step(): jnp.einsum('sbcd,sbd->sbc', picked, hidden_all, preferred_element_type=jn...  19.4 us
    gather x1, local copies, waits for them, and re-layouts, local_step(): scores = back_scores[safe_owner, row_idx, slot_rank] / value_a11  17.5 us
    unnamed x12, local copies, waits for them, and re-layouts  9.79 us
  transfers between devices with their start and end apart: 3, of which 2 were waited for; matrix products, arithmetic and copies ran while one was open for 40% of the time, Pallas kernels for 0%

commit v1 on v0

v1 whole, which is shorter than its diff:
```python
import functools

import jax
import jax.numpy as jnp
from jax import lax
from jax.experimental import pallas as pl
from jax.experimental.pallas import tpu as pltpu
from jax.sharding import PartitionSpec as P

MESH = pl.DeviceIdType.MESH
TEMP = 0.5
CAP = 16
GROUP = 8
DEPTH = 6


def entry_barrier(n_model, n_vocab, m, v):
    barrier = pltpu.get_barrier_semaphore()
    for dm in range(n_model):
        for dv in range(n_vocab):
            if dm or dv:
                pl.semaphore_signal(
                    barrier, inc=1,
                    device_id={"model": lax.rem(m + dm, n_model), "vocab": lax.rem(v + dv, n_vocab)},
                    device_id_type=MESH,
                )
    return barrier


def route_kernel(shard_len, n_model, n_vocab, h_ref, ids_ref, valid_ref, tgt_ref, tbl_ref, hall_ref, meta_ref,
                 t_ref, send_ref, tin_ref, hbuf, tsend, trecv, hsend, hrecv, lsem):
    n = n_model * n_vocab
    rows, length = ids_ref.shape
    m, v = lax.axis_index("model"), lax.axis_index("vocab")
    me = m * n_vocab + v
    barrier = entry_barrier(n_model, n_vocab, m, v)

    ids = ids_ref[...]
    ok = valid_ref[...] > 0
    owner = jnp.where(ok, lax.div(ids, shard_len), n)
    off = lax.rem(ids, shard_len)
    tri = (lax.broadcasted_iota(jnp.int32, (length, length), 0)
           < lax.broadcasted_iota(jnp.int32, (length, length), 1)).astype(jnp.bfloat16)
    rank = jnp.zeros((rows, length), jnp.float32)
    for s in range(n):
        hit = owner == s
        count = jnp.dot(jnp.where(hit, 1.0, 0.0).astype(jnp.bfloat16), tri, preferred_element_type=jnp.float32)
        rank = rank + jnp.where(hit, count, 0.0)
    rank = rank.astype(jnp.int32)
    slot = jnp.where(ok, owner * CAP + rank, n * CAP)
    pair = off - lax.rem(off, 2)

    lane = lax.broadcasted_iota(jnp.int32, (rows, n * CAP), 1)
    row = lax.broadcasted_iota(jnp.int32, (rows, n * CAP), 0)
    spread = lax.rem(((me * rows + row) * CAP + lax.rem(lane, CAP)) * 4, shard_len)
    table = spread
    for j in range(length):
        table = jnp.where(lane == slot[:, j:j + 1], pair[:, j:j + 1], table)
    t_ref[...] = table

    code = jnp.where(ok, owner * (2 * CAP) + rank * 2 + lax.rem(off, 2), -1)
    diag = (lax.broadcasted_iota(jnp.int32, (rows, rows), 0) == lax.broadcasted_iota(jnp.int32, (rows, rows), 1))
    tcol = jnp.sum(jnp.where(diag, tgt_ref[...].reshape(1, rows), 0).astype(jnp.float32), axis=1, keepdims=True)
    meta_ref[:, :length] = code
    meta_ref[:, length:] = jnp.broadcast_to(tcol.astype(jnp.int32), (rows, length))

    groups = 128 // CAP
    per = rows // groups
    lane4 = lax.broadcasted_iota(jnp.int32, (per, 128), 1)
    parts = [jnp.zeros((per, 128), jnp.int32) for _ in range(n)]
    for q in range(groups):
        tq = t_ref[pl.ds(q, per, stride=groups), :]
        inside = lax.div(lane4, CAP) == q
        for s in range(n):
            moved = tq if q == s else pltpu.roll(tq, ((q - s) * CAP) % 128, axis=1)
            parts[s] = jnp.where(inside, moved, parts[s])
    for s in range(n):
        send_ref[s] = parts[s]

    pl.semaphore_wait(barrier, n - 1)

    def remote(src, dst, k, to):
        return pltpu.make_async_remote_copy(src_ref=src, dst_ref=dst, send_sem=hsend.at[k], recv_sem=hrecv.at[k],
                                            device_id=to, device_id_type=MESH)

    def at(mm, vv):
        return {"model": mm, "vocab": vv}

    tcopies = []
    for k in range(1, n):
        dm, dv = k // n_vocab, k % n_vocab
        om, ov = lax.rem(m + dm, n_model), lax.rem(v + dv, n_vocab)
        c = pltpu.make_async_remote_copy(
            src_ref=send_ref.at[om * n_vocab + ov], dst_ref=tin_ref.at[me], send_sem=tsend.at[k], recv_sem=trecv.at[k],
            device_id=at(om, ov), device_id_type=MESH)
        c.start()
        tcopies.append(c)

    core = lax.rem(v, 2)
    xpos = lax.div(v, 2)
    vp = xpos * 2 + (1 - core)
    vx = (1 - xpos) * 2 + core
    my = 1 - m
    partner, xpeer, ypeer = at(m, vp), at(m, vx), at(my, v)
    ix, iy, idg = m * n_vocab + vx, my * n_vocab + v, my * n_vocab + vx
    half = rows // 2
    lo, hi = pl.ds(0, half), pl.ds(half, half)

    own_x = [remote(h_ref.at[lo], hbuf.at[me, lo], 0, xpeer), remote(h_ref.at[hi], hbuf.at[me, hi], 1, xpeer)]
    own_y = [remote(h_ref.at[lo], hbuf.at[me, lo], 2, ypeer), remote(h_ref.at[hi], hbuf.at[me, hi], 3, ypeer)]
    own_p = remote(h_ref, hbuf.at[me], 4, partner)
    x_to_y = remote(hbuf.at[ix, lo], hbuf.at[ix, lo], 5, ypeer)
    y_to_x = remote(hbuf.at[iy, hi], hbuf.at[iy, hi], 6, xpeer)
    x_p = [remote(hbuf.at[ix, lo], hbuf.at[ix, lo], 7, partner), remote(hbuf.at[ix, hi], hbuf.at[ix, hi], 8, partner)]
    y_p = [remote(hbuf.at[iy, lo], hbuf.at[iy, lo], 9, partner), remote(hbuf.at[iy, hi], hbuf.at[iy, hi], 10, partner)]
    d_p = [remote(hbuf.at[idg, lo], hbuf.at[idg, lo], 11, partner), remote(hbuf.at[idg, hi], hbuf.at[idg, hi], 12, partner)]

    own_x[0].start()
    own_y[1].start()
    own_x[1].start()
    own_y[0].start()
    own_p.start()
    keep = pltpu.make_async_copy(h_ref, hall_ref.at[me], lsem.at[0])
    keep.start()
    tbl_ref[me] = send_ref[me]

    own_x[0].wait_recv()
    x_to_y.start()
    x_p[0].start()
    own_y[1].wait_recv()
    y_to_x.start()
    y_p[1].start()
    own_p.wait_recv()
    out = [pltpu.make_async_copy(hbuf.at[m * n_vocab + vp], hall_ref.at[m * n_vocab + vp], lsem.at[1])]
    out[0].start()
    own_x[1].wait_recv()
    x_p[1].start()
    own_y[0].wait_recv()
    y_p[0].start()
    for k in range(1, n):
        tcopies[k - 1].wait_recv()
    for s in range(n):
        @pl.when(s != me)
        def _():
            tbl_ref[s] = tin_ref[s]

    def keep_block(slot, sem):
        c = pltpu.make_async_copy(hbuf.at[slot], hall_ref.at[slot], lsem.at[sem])
        c.start()
        out.append(c)

    keep_block(ix, 2)
    keep_block(iy, 3)
    x_to_y.wait_recv()
    d_p[0].start()
    y_to_x.wait_recv()
    d_p[1].start()
    keep_block(idg, 4)
    for c in x_p:
        c.wait_recv()
    keep_block(m * n_vocab + (1 - xpos) * 2 + (1 - core), 5)
    for c in y_p:
        c.wait_recv()
    keep_block(my * n_vocab + vp, 6)
    for c in d_p:
        c.wait_recv()
    keep_block(my * n_vocab + (1 - xpos) * 2 + (1 - core), 7)
    for c in tcopies + own_x + own_y + [own_p, x_to_y, y_to_x] + x_p + y_p + d_p:
        c.wait_send()
    keep.wait()
    for c in out:
        c.wait()


def score_kernel(chunks, tbl_ref, h_hbm, w_hbm, out_ref, buf, h_ref, sems, hsem):
    slots = 128

    hcopy = pltpu.make_async_copy(h_hbm, h_ref, hsem)
    hcopy.start()

    def issue(c, b):
        def body(g, _):
            for u in range(16):
                k = g * 16 + u
                at = pl.multiple_of(tbl_ref[c, k], 2)
                pltpu.make_async_copy(
                    w_hbm.at[pl.ds(at, 2), :], buf.at[b, pl.ds(pl.multiple_of(2 * k, 2), 2), :], sems.at[b]
                ).start(priority=u % 2)
            return 0
        lax.fori_loop(0, slots // 16, body, 0)

    for c in range(DEPTH - 1):
        issue(c, c)
    hcopy.wait()

    lane = lax.broadcasted_iota(jnp.int32, (GROUP, 2 * slots), 1)
    row = lax.broadcasted_iota(jnp.int32, (GROUP, 2 * slots), 0)
    mine = lax.div(lane, 2 * CAP) == row

    def step(c, _):
        b = lax.rem(c, DEPTH)

        @pl.when(c + DEPTH - 1 < chunks)
        def _():
            issue(c + DEPTH - 1, lax.rem(c + DEPTH - 1, DEPTH))

        pltpu.make_async_copy(w_hbm.at[pl.ds(0, 2 * slots), :], buf.at[b], sems.at[b]).wait()
        hs = h_ref[c]
        part = lax.dot_general(hs, buf[b], (((1,), (1,)), ((), ())), preferred_element_type=jnp.float32)
        out_ref[pl.ds(c, 1), :] = jnp.sum(jnp.where(mine, part, 0.0), axis=0, keepdims=True)
        return 0

    lax.fori_loop(0, chunks, step, 0)


def finish_kernel(n_model, n_vocab, sc_ref, meta_ref, p_ref, lp_ref, inb, wide0, wide1, ssend, srecv):
    n = n_model * n_vocab
    wide = (wide0, wide1)
    rows, length = p_ref.shape
    m, v = lax.axis_index("model"), lax.axis_index("vocab")
    me = m * n_vocab + v
    barrier = entry_barrier(n_model, n_vocab, m, v)
    pl.semaphore_wait(barrier, n - 1)
    copies = []
    for k in range(1, n):
        om, ov = lax.rem(m + k // n_vocab, n_model), lax.rem(v + k % n_vocab, n_vocab)
        c = pltpu.make_async_remote_copy(
            src_ref=sc_ref.at[om * n_vocab + ov], dst_ref=inb.at[me], send_sem=ssend.at[k], recv_sem=srecv.at[k],
            device_id={"model": om, "vocab": ov}, device_id_type=MESH)
        c.start()
        copies.append(c)
    inb[me] = sc_ref[me]
    for c in copies:
        c.wait_recv()
    width = 2 * CAP
    groups = rows // GROUP
    lane = lax.broadcasted_iota(jnp.int32, (groups, 128), 1)
    per = 128 // width
    for q in range(GROUP):
        for hb in range(2):
            acc = jnp.zeros((groups, 128), jnp.float32)
            for sl in range(per):
                s = hb * per + sl
                src = inb[s][:, (q // per) * 128:(q // per + 1) * 128]
                shift = ((sl - q % per) * width) % 128
                moved = pltpu.roll(src, shift, axis=1) if shift else src
                acc = jnp.where(lax.div(lane, width) == sl, moved, acc)
            wide[hb][pl.ds(q, groups, stride=GROUP), :] = acc
    meta = meta_ref[...]
    code = meta[:, :length]
    ok = code >= 0
    full = jnp.concatenate([jnp.where(ok, code, 0), jnp.zeros((rows, 128 - length), jnp.int32)], axis=1)
    low = jnp.take_along_axis(wide0[...], lax.rem(full, 128), axis=1)
    high = jnp.take_along_axis(wide1[...], lax.rem(full, 128), axis=1)
    scores = jnp.where(full < 128, low, high)[:, :length] / TEMP
    scores = jnp.where(ok, scores, -jnp.inf)
    top = jnp.max(scores, axis=1, keepdims=True)
    log_norm = top + jnp.log(jnp.sum(jnp.exp(scores - top), axis=1, keepdims=True))
    p_ref[...] = jnp.where(ok, jnp.exp(scores - log_norm), 0.0)
    at = lax.broadcasted_iota(jnp.int32, (rows, length), 1)
    picked = jnp.sum(jnp.where(at == meta[:, length:], scores, 0.0), axis=1, keepdims=True)
    diag = (lax.broadcasted_iota(jnp.int32, (rows, rows), 0) == lax.broadcasted_iota(jnp.int32, (rows, rows), 1))
    lp_ref[...] = jnp.sum(jnp.where(diag, picked - log_norm, 0.0), axis=0)
    for c in copies:
        c.wait_send()


def solution(mesh):
    axes = ("model", "vocab")
    n_model, n_vocab = mesh.shape["model"], mesh.shape["vocab"]
    n = n_model * n_vocab
    row_spec = P(("rep",) + axes, None)
    vec_spec = P(("rep",) + axes)
    vmem = pl.BlockSpec(memory_space=pltpu.VMEM)
    hbm = pl.BlockSpec(memory_space=pl.ANY)
    smem = pl.BlockSpec(memory_space=pltpu.SMEM)

    def local_step(hidden, head_rows, allowed_ids, valid_mask, target_pos):
        rows, length = allowed_ids.shape
        shard_len, width = head_rows.shape
        per = rows * CAP // 128
        tbl, hall, meta = pl.pallas_call(
            functools.partial(route_kernel, shard_len, n_model, n_vocab),
            out_shape=(jax.ShapeDtypeStruct((n, per, 128), jnp.int32),
                       jax.ShapeDtypeStruct((n, rows, width), jnp.bfloat16),
                       jax.ShapeDtypeStruct((rows, 2 * length), jnp.int32)),
            in_specs=[vmem, vmem, vmem, vmem],
            out_specs=(vmem, hbm, vmem),
            scratch_shapes=[
                pltpu.VMEM((rows, n * CAP), jnp.int32),
                pltpu.VMEM((n, per, 128), jnp.int32),
                pltpu.VMEM((n, per, 128), jnp.int32),
                pltpu.VMEM((n, rows, width), jnp.bfloat16),
                pltpu.SemaphoreType.DMA((n,)),
                pltpu.SemaphoreType.DMA((n,)),
                pltpu.SemaphoreType.DMA((13,)),
                pltpu.SemaphoreType.DMA((13,)),
                pltpu.SemaphoreType.DMA((n,)),
            ],
            compiler_params=pltpu.CompilerParams(collective_id=0, has_side_effects=True),
            name="route",
        )(hidden, allowed_ids, valid_mask, target_pos)
        chunks = n * rows // GROUP
        scores = pl.pallas_call(
            functools.partial(score_kernel, chunks),
            out_shape=jax.ShapeDtypeStruct((chunks, 256), jnp.float32),
            in_specs=[smem, hbm, hbm],
            out_specs=vmem,
            scratch_shapes=[
                pltpu.VMEM((DEPTH, 256, width), jnp.bfloat16),
                pltpu.VMEM((chunks, GROUP, width), jnp.bfloat16),
                pltpu.SemaphoreType.DMA((DEPTH,)),
                pltpu.SemaphoreType.DMA,
            ],
            compiler_params=pltpu.CompilerParams(vmem_limit_bytes=48 * 1024 * 1024),
            name="score",
        )(tbl.reshape(n * per, 128), hall.reshape(chunks, GROUP, width), head_rows)
        probs, lp = pl.pallas_call(
            functools.partial(finish_kernel, n_model, n_vocab),
            out_shape=(jax.ShapeDtypeStruct((rows, length), jnp.float32), jax.ShapeDtypeStruct((rows,), jnp.float32)),
            in_specs=[vmem, vmem],
            out_specs=(vmem, vmem),
            scratch_shapes=[
                pltpu.VMEM((n, rows // GROUP, 256), jnp.float32),
                pltpu.VMEM((rows, 128), jnp.float32),
                pltpu.VMEM((rows, 128), jnp.float32),
                pltpu.SemaphoreType.DMA((n,)),
                pltpu.SemaphoreType.DMA((n,)),
            ],
            compiler_params=pltpu.CompilerParams(collective_id=1, has_side_effects=True),
            name="finish",
        )(scores.reshape(n, rows // GROUP, 256), meta)
        return probs, lp

    return jax.shard_map(local_step, mesh=mesh, in_specs=(row_spec, P(axes, None), row_spec, row_spec, vec_spec),
                         out_specs=(row_spec, vec_spec), check_vma=False)
```

time: 429 us -> 97 us (0.23); the launches traced: 422 us -> 96.7 us
  starting transfers between devices: 190 us -> 0 us
  local copies, waits for them, and re-layouts: 182 us -> 5.58 us
  Pallas kernels: 0 us -> 90.4 us
  matrix products: 19.4 us -> 0 us
  between operations: 14.2 us -> 0.66 us
  waiting for transfers between devices: 9.16 us -> 0 us
  other arithmetic: 7.54 us -> 0 us
    all_to_all x2 -> x0, starting transfers between devices: 189 us -> none  [the longest x1 185 us: local_step(): back_scores = lax.all_to_all(part_scores, shard_axes, 0, 0)]
    gather x3 -> x0, local copies, waits for them, and re-layouts: 171 us -> none  [the longest x1 152 us: local_step(): picked = head_rows[recv_ids]]
    pallas_call x0 -> x3, Pallas kernels: none -> 90.4 us  [the longest x1 63.3 us: local_step(): pl.pallas_call(functools.partial(score_kernel, chunks), out_shape=jax.Sha...]
    dot_general x1 -> x0, matrix products: 19.4 us -> none  [local_step(): jnp.einsum('sbcd,sbd->sbc', picked, hidden_all, preferred_element_type=jn...]
    all_to_all x2 -> x0, waiting for transfers between devices: 8.48 us -> none  [the longest x1 4.46 us: local_step(): back_scores = lax.all_to_all(part_scores, shard_axes, 0, 0)]
    unnamed x12 -> x6, local copies, waits for them, and re-layouts: 9.79 us -> 4.96 us
  transfers between devices with their start and end apart: 3 -> 0, of which waited for: 2 -> 0; matrix products, arithmetic and copies ran while one was open for 40% -> 0% of each run, Pallas kernels for 0% -> 0%
where the time goes in v1:
time: 97 us; the launch traced here: 96.7 us
  Pallas kernels  90.4 us (93%)
  local copies, waits for them, and re-layouts  5.58 us (6%)
    pallas_call x1, Pallas kernels, local_step(): pl.pallas_call(functools.partial(score_kernel, chunks), out_shape=jax.Sha...  63.3 us
    pallas_call x1, Pallas kernels, local_step(): pl.pallas_call(functools.partial(route_kernel, shard_len, n_model, n_voca...  20 us
    pallas_call x1, Pallas kernels, local_step(): pl.pallas_call(functools.partial(finish_kernel, n_model, n_vocab), out_sh...  7.08 us
    unnamed x6, local copies, waits for them, and re-layouts  4.96 us

profile of v1, /device:TPU:0, one launch (start us, length us, event | category | flops | bytes accessed | tf_op | source)
XLA Modules:
  0.0 96.7 jit_solution(14044280078707799285)
XLA Ops:
  0.6 20.0 %route.1 = (s32[8,4,128]{2,1,0:T(4,128)}, bf16[8,32,5120]{2,1,0:T(8,128)(2,1)}, s32[32,128]{1,0:T(8,128)}) custom-call(bf16[32,5120]{1,0:T(8,128)(2,1)} %h_ref.1, s32[32,64]{1,0:T(8,128)} %ids_ref.1, s32[32,64]{1,0:T(8,128)} %valid_ref.1, s32[32]{0:T(128)} %tgt_ref.1), custom_call_target="tpu_custom_call" | custom-call | tf_op jit(solution)/shard_map/route/pallas_call | solution.py:282
  20.6 0.0 copy-start
  20.7 1.7 %copy-done = bf16[8,32,5120]{2,1,0:T(8,128)(2,1)S(1)} copy-done((bf16[8,32,5120]{2,1,0:T(8,128)(2,1)S(1)}, bf16[8,32,5120]{2,1,0:T(8,128)(2,1)}, u32[]{:S(2)}) %copy-start) | copy-done | bytes 2621464
  22.4 0.0 copy-start.1
  22.4 0.7 copy-done.1
  23.1 63.3 %score.1 = f32[32,256]{1,0:T(8,128)S(1)} custom-call(s32[32,128]{1,0:T(8,128)S(1)} %bitcast.3, bf16[32,8,5120]{2,1,0:T(8,128)(2,1)S(1)} %bitcast.2, bf16[16384,5120]{1,0:T(8,128)(2,1)} %w_hbm.1), custom_call_target="tpu_custom_call" | custom-call | tf_op jit(solution)/shard_map/score/pallas_call | solution.py:304
  86.4 0.6 reshape.15.sc_ref
  87.1 7.1 %finish.1 = (f32[32,64]{1,0:T(8,128)}, f32[32]{0:T(128)}) custom-call(f32[8,4,256]{2,1,0:T(4,128)} %reshape.15.sc_ref, s32[32,128]{1,0:T(8,128)} %get-tuple-element.7.meta_ref), custom_call_target="tpu_custom_call" | custom-call | tf_op jit(solution)/shard_map/finish/pallas_call | solution.py:318
  94.1 1.3 %copy.9 = f32[32,64]{1,0:T(8,128)} copy(f32[32,64]{1,0:T(8,128)} %get-tuple-element.10) | data formatting | bytes 16384
  95.5 1.2 %copy.10 = f32[32]{0:T(128)} copy(f32[32]{0:T(128)} %get-tuple-element.11) | data formatting | bytes 256
Async XLA Ops:
  20.6 1.7 %copy-start = (bf16[8,32,5120]{2,1,0:T(8,128)(2,1)S(1)}, bf16[8,32,5120]{2,1,0:T(8,128)(2,1)}, u32[]{:S(2)}) copy-start(bf16[8,32,5120]{2,1,0:T(8,128)(2,1)} %get-tuple-element.6) | copy-start | bytes 7864324
  22.4 0.7 copy-start.1

commit v2 on v1

--- a/solution.py
+++ b/solution.py
@@ -11,7 +11,8 @@
 TEMP = 0.5
 CAP = 16
 GROUP = 8
-DEPTH = 6
+DEPTH = 4
+PIECES = 4
 
 
 def entry_barrier(n_model, n_vocab, m, v):
@@ -172,45 +173,48 @@
         c.wait()
 
 
-def score_kernel(chunks, tbl_ref, h_hbm, w_hbm, out_ref, buf, h_ref, sems, hsem):
+def score_kernel(chunks, pieces, tbl_ref, h_hbm, w_hbm, out_ref, *scratch):
+    bufs, (h_ref, sems, hsem) = scratch[:DEPTH], scratch[DEPTH:]
     slots = 128
+    width = w_hbm.shape[1]
 
     hcopy = pltpu.make_async_copy(h_hbm, h_ref, hsem)
     hcopy.start()
 
-    def issue(c, b):
-        def body(g, _):
-            for u in range(16):
-                k = g * 16 + u
-                at = pl.multiple_of(tbl_ref[c, k], 2)
-                pltpu.make_async_copy(
-                    w_hbm.at[pl.ds(at, 2), :], buf.at[b, pl.ds(pl.multiple_of(2 * k, 2), 2), :], sems.at[b]
-                ).start(priority=u % 2)
-            return 0
-        lax.fori_loop(0, slots // 16, body, 0)
+    def issue(c, b, lo=0, hi=slots):
+        for k in range(lo, hi):
+            at = pl.multiple_of(tbl_ref[c, k], 2)
+            pltpu.make_async_copy(
+                w_hbm.at[pl.ds(at, 2), :], bufs[b].at[pl.ds(2 * k, 2), :], sems.at[b]
+            ).start(priority=k % 2)
+
+    lane = lax.broadcasted_iota(jnp.int32, (GROUP, 2 * slots), 1)
+    row = lax.broadcasted_iota(jnp.int32, (GROUP, 2 * slots), 0)
+    mine = lax.div(lane, 2 * CAP) == row
+
+    def work(c, b, more):
+        pltpu.make_async_copy(w_hbm.at[pl.ds(0, 2 * slots), :], bufs[b], sems.at[b]).wait()
+        part = jnp.zeros((GROUP, 2 * slots), jnp.float32)
+        for q in range(pieces):
+            if more:
+                issue(c + DEPTH - 1, (b + DEPTH - 1) % DEPTH, q * slots // pieces, (q + 1) * slots // pieces)
+            ks = slice(q * width // pieces, (q + 1) * width // pieces)
+            part = part + lax.dot_general(h_ref[c, :, ks], bufs[b][:, ks], (((1,), (1,)), ((), ())),
+                                          preferred_element_type=jnp.float32)
+        out_ref[pl.ds(c, 1), :] = jnp.sum(jnp.where(mine, part, 0.0), axis=0, keepdims=True)
 
     for c in range(DEPTH - 1):
         issue(c, c)
     hcopy.wait()
 
-    lane = lax.broadcasted_iota(jnp.int32, (GROUP, 2 * slots), 1)
-    row = lax.broadcasted_iota(jnp.int32, (GROUP, 2 * slots), 0)
-    mine = lax.div(lane, 2 * CAP) == row
-
-    def step(c, _):
-        b = lax.rem(c, DEPTH)
-
-        @pl.when(c + DEPTH - 1 < chunks)
-        def _():
-            issue(c + DEPTH - 1, lax.rem(c + DEPTH - 1, DEPTH))
-
-        pltpu.make_async_copy(w_hbm.at[pl.ds(0, 2 * slots), :], buf.at[b], sems.at[b]).wait()
-        hs = h_ref[c]
-        part = lax.dot_general(hs, buf[b], (((1,), (1,)), ((), ())), preferred_element_type=jnp.float32)
-        out_ref[pl.ds(c, 1), :] = jnp.sum(jnp.where(mine, part, 0.0), axis=0, keepdims=True)
+    def step(g, _):
+        for b in range(DEPTH):
+            work(g * DEPTH + b, b, True)
         return 0
 
-    lax.fori_loop(0, chunks, step, 0)
+    lax.fori_loop(0, chunks // DEPTH - 1, step, 0)
+    for b in range(DEPTH):
+        work(chunks - DEPTH + b, b, b == 0)
 
 
 def finish_kernel(n_model, n_vocab, sc_ref, meta_ref, p_ref, lp_ref, inb, wide0, wide1, ssend, srecv):
@@ -302,12 +306,12 @@
         )(hidden, allowed_ids, valid_mask, target_pos)
         chunks = n * rows // GROUP
         scores = pl.pallas_call(
-            functools.partial(score_kernel, chunks),
+            functools.partial(score_kernel, chunks, PIECES),
             out_shape=jax.ShapeDtypeStruct((chunks, 256), jnp.float32),
             in_specs=[smem, hbm, hbm],
             out_specs=vmem,
             scratch_shapes=[
-                pltpu.VMEM((DEPTH, 256, width), jnp.bfloat16),
+                *[pltpu.VMEM((256, width), jnp.bfloat16)] * DEPTH,
                 pltpu.VMEM((chunks, GROUP, width), jnp.bfloat16),
                 pltpu.SemaphoreType.DMA((DEPTH,)),
                 pltpu.SemaphoreType.DMA,

time: 97 us -> 86.9 us (0.90)
  Pallas kernels: 90.4 us -> 80.3 us
    pallas_call x1, Pallas kernels: 63.3 us -> 53.2 us  [local_step(): pl.pallas_call(functools.partial(score_kernel, chunks, PIECES), out_shape...]
where the time goes in v2:
time: 86.9 us; the launch traced here: 86.6 us
  Pallas kernels  80.3 us (92%)
  local copies, waits for them, and re-layouts  5.58 us (6%)
    pallas_call x1, Pallas kernels, local_step(): pl.pallas_call(functools.partial(score_kernel, chunks, PIECES), out_shape...  53.2 us
    pallas_call x1, Pallas kernels, local_step(): pl.pallas_call(functools.partial(route_kernel, shard_len, n_model, n_voca...  20 us
    pallas_call x1, Pallas kernels, local_step(): pl.pallas_call(functools.partial(finish_kernel, n_model, n_vocab), out_sh...  7.08 us
    unnamed x6, local copies, waits for them, and re-layouts  4.96 us

profile of v2, /device:TPU:0, one launch (start us, length us, event | category | flops | bytes accessed | tf_op | source)
XLA Modules:
  0.0 86.6 jit_solution(14744075391656544538)
XLA Ops:
  0.6 20.0 %route.1 = (s32[8,4,128]{2,1,0:T(4,128)}, bf16[8,32,5120]{2,1,0:T(8,128)(2,1)}, s32[32,128]{1,0:T(8,128)}) custom-call(bf16[32,5120]{1,0:T(8,128)(2,1)} %h_ref.1, s32[32,64]{1,0:T(8,128)} %ids_ref.1, s32[32,64]{1,0:T(8,128)} %valid_ref.1, s32[32]{0:T(128)} %tgt_ref.1), custom_call_target="tpu_custom_call" | custom-call | tf_op jit(solution)/shard_map/route/pallas_call | solution.py:286
  20.6 0.0 copy-start
  20.7 1.7 %copy-done = bf16[8,32,5120]{2,1,0:T(8,128)(2,1)S(1)} copy-done((bf16[8,32,5120]{2,1,0:T(8,128)(2,1)S(1)}, bf16[8,32,5120]{2,1,0:T(8,128)(2,1)}, u32[]{:S(2)}) %copy-start) | copy-done | bytes 2621464
  22.4 0.0 copy-start.1
  22.4 0.7 copy-done.1
  23.1 53.2 %score.1 = f32[32,256]{1,0:T(8,128)S(1)} custom-call(s32[32,128]{1,0:T(8,128)S(1)} %bitcast.3, bf16[32,8,5120]{2,1,0:T(8,128)(2,1)S(1)} %bitcast.2, bf16[16384,5120]{1,0:T(8,128)(2,1)} %w_hbm.1), custom_call_target="tpu_custom_call" | custom-call | tf_op jit(solution)/shard_map/score/pallas_call | solution.py:308
  76.3 0.6 reshape.15.sc_ref
  77.0 7.1 %finish.1 = (f32[32,64]{1,0:T(8,128)}, f32[32]{0:T(128)}) custom-call(f32[8,4,256]{2,1,0:T(4,128)} %reshape.15.sc_ref, s32[32,128]{1,0:T(8,128)} %get-tuple-element.7.meta_ref), custom_call_target="tpu_custom_call" | custom-call | tf_op jit(solution)/shard_map/finish/pallas_call | solution.py:322
  84.0 1.3 %copy.9 = f32[32,64]{1,0:T(8,128)} copy(f32[32,64]{1,0:T(8,128)} %get-tuple-element.10) | data formatting | bytes 16384
  85.4 1.2 %copy.10 = f32[32]{0:T(128)} copy(f32[32]{0:T(128)} %get-tuple-element.11) | data formatting | bytes 256
Async XLA Ops:
  20.6 1.7 %copy-start = (bf16[8,32,5120]{2,1,0:T(8,128)(2,1)S(1)}, bf16[8,32,5120]{2,1,0:T(8,128)(2,1)}, u32[]{:S(2)}) copy-start(bf16[8,32,5120]{2,1,0:T(8,128)(2,1)} %get-tuple-element.6) | copy-start | bytes 7864324
  22.4 0.7 copy-start.1

commit v3 on v2

--- a/solution.py
+++ b/solution.py
@@ -10,9 +10,8 @@
 MESH = pl.DeviceIdType.MESH
 TEMP = 0.5
 CAP = 16
-GROUP = 8
+SLOTS = 128
 DEPTH = 4
-PIECES = 4
 
 
 def entry_barrier(n_model, n_vocab, m, v):
@@ -59,7 +58,8 @@
         table = jnp.where(lane == slot[:, j:j + 1], pair[:, j:j + 1], table)
     t_ref[...] = table
 
-    code = jnp.where(ok, owner * (2 * CAP) + rank * 2 + lax.rem(off, 2), -1)
+    code = lax.div(rank, 4) * (n * 8) + owner * 8 + lax.rem(rank, 4) * 2 + lax.rem(off, 2)
+    code = jnp.where(ok, code, -1)
     diag = (lax.broadcasted_iota(jnp.int32, (rows, rows), 0) == lax.broadcasted_iota(jnp.int32, (rows, rows), 1))
     tcol = jnp.sum(jnp.where(diag, tgt_ref[...].reshape(1, rows), 0).astype(jnp.float32), axis=1, keepdims=True)
     meta_ref[:, :length] = code
@@ -173,38 +173,50 @@
         c.wait()
 
 
-def score_kernel(chunks, pieces, tbl_ref, h_hbm, w_hbm, out_ref, *scratch):
-    bufs, (h_ref, sems, hsem) = scratch[:DEPTH], scratch[DEPTH:]
-    slots = 128
-    width = w_hbm.shape[1]
+def score_kernel(chunks, tbl_ref, h_hbm, w_hbm, out_ref, *scratch):
+    bufs, (h_ref, hf_ref, sems, hsem) = scratch[:DEPTH], scratch[DEPTH:]
+    tiles = w_hbm.shape[1]
+    nrow = SLOTS // CAP
+    quads = CAP // 4
 
     hcopy = pltpu.make_async_copy(h_hbm, h_ref, hsem)
     hcopy.start()
 
-    def issue(c, b, lo=0, hi=slots):
-        for k in range(lo, hi):
-            at = pl.multiple_of(tbl_ref[c, k], 2)
-            pltpu.make_async_copy(
-                w_hbm.at[pl.ds(at, 2), :], bufs[b].at[pl.ds(2 * k, 2), :], sems.at[b]
-            ).start(priority=k % 2)
-
-    lane = lax.broadcasted_iota(jnp.int32, (GROUP, 2 * slots), 1)
-    row = lax.broadcasted_iota(jnp.int32, (GROUP, 2 * slots), 0)
-    mine = lax.div(lane, 2 * CAP) == row
+    def issue(c, b, k):
+        at = tbl_ref[c, k]
+        t, p = lax.shift_right_logical(at, 3), lax.bitwise_and(lax.shift_right_logical(at, 1), 3)
+        pltpu.make_async_copy(
+            w_hbm.at[t, :, p], bufs[b].at[k // 4, :, pl.ds(2 * (k % 4), 2), :], sems.at[b]).start(priority=k % 2)
+
+    lane = lax.broadcasted_iota(jnp.int32, (8, 128), 1)
 
     def work(c, b, more):
-        pltpu.make_async_copy(w_hbm.at[pl.ds(0, 2 * slots), :], bufs[b], sems.at[b]).wait()
-        part = jnp.zeros((GROUP, 2 * slots), jnp.float32)
-        for q in range(pieces):
-            if more:
-                issue(c + DEPTH - 1, (b + DEPTH - 1) % DEPTH, q * slots // pieces, (q + 1) * slots // pieces)
-            ks = slice(q * width // pieces, (q + 1) * width // pieces)
-            part = part + lax.dot_general(h_ref[c, :, ks], bufs[b][:, ks], (((1,), (1,)), ((), ())),
-                                          preferred_element_type=jnp.float32)
-        out_ref[pl.ds(c, 1), :] = jnp.sum(jnp.where(mine, part, 0.0), axis=0, keepdims=True)
+        pltpu.make_async_copy(bufs[b], bufs[b], sems.at[b]).wait()
+        flat = bufs[b].reshape(SLOTS // 4 * tiles * 8, 128)
+        hf_ref[...] = h_ref[c].astype(jnp.float32)
+        got = jnp.zeros((8, 128), jnp.float32)
+        base = lax.rem(c, 128 // (SLOTS // 4)) * (SLOTS // 4)
+        for i in range(nrow):
+            acc = [[jnp.zeros((8, 128), jnp.float32)] * 2 for _ in range(quads)]
+            for kk in range(0, tiles, 2):
+                if more:
+                    for k in range(-(-kk * CAP // tiles), -(-(kk + 2) * CAP // tiles)):
+                        issue(c + DEPTH - 1, (b + DEPTH - 1) % DEPTH, i * CAP + k)
+                hb = [jnp.broadcast_to(hf_ref[i:i + 1, (kk + z) * 128:(kk + z + 1) * 128], (8, 128)) for z in (0, 1)]
+                for g in range(quads):
+                    at = ((i * quads + g) * tiles + kk) * 8
+                    x = flat[at:at + 16, :].astype(jnp.float32)
+                    acc[g] = [acc[g][0] + x[:8] * hb[0], acc[g][1] + x[8:] * hb[1]]
+            for g in range(quads):
+                total = jnp.sum(acc[g][0] + acc[g][1], axis=1, keepdims=True)
+                got = jnp.where(lane == base + (i * quads + g), total, got)
+        at = lax.div(c, 128 // (SLOTS // 4))
+        fresh = (lane >= base) & (lane < base + SLOTS // 4)
+        out_ref[at] = jnp.where(fresh, got, out_ref[at])
 
     for c in range(DEPTH - 1):
-        issue(c, c)
+        for k in range(SLOTS):
+            issue(c, c, k)
     hcopy.wait()
 
     def step(g, _):
@@ -217,9 +229,8 @@
         work(chunks - DEPTH + b, b, b == 0)
 
 
-def finish_kernel(n_model, n_vocab, sc_ref, meta_ref, p_ref, lp_ref, inb, wide0, wide1, ssend, srecv):
+def finish_kernel(n_model, n_vocab, sc_ref, meta_ref, p_ref, lp_ref, inb, flip, ssend, srecv):
     n = n_model * n_vocab
-    wide = (wide0, wide1)
     rows, length = p_ref.shape
     m, v = lax.axis_index("model"), lax.axis_index("vocab")
     me = m * n_vocab + v
@@ -236,26 +247,14 @@
     inb[me] = sc_ref[me]
     for c in copies:
         c.wait_recv()
-    width = 2 * CAP
-    groups = rows // GROUP
-    lane = lax.broadcasted_iota(jnp.int32, (groups, 128), 1)
-    per = 128 // width
-    for q in range(GROUP):
-        for hb in range(2):
-            acc = jnp.zeros((groups, 128), jnp.float32)
-            for sl in range(per):
-                s = hb * per + sl
-                src = inb[s][:, (q // per) * 128:(q // per + 1) * 128]
-                shift = ((sl - q % per) * width) % 128
-                moved = pltpu.roll(src, shift, axis=1) if shift else src
-                acc = jnp.where(lax.div(lane, width) == sl, moved, acc)
-            wide[hb][pl.ds(q, groups, stride=GROUP), :] = acc
+    flip[...] = inb[...].reshape(n * 8, 128).T
+    wide = [jnp.concatenate([flip[pl.ds(q, rows, stride=4), :] for q in (2 * hb, 2 * hb + 1)], axis=1) for hb in (0, 1)]
     meta = meta_ref[...]
     code = meta[:, :length]
     ok = code >= 0
     full = jnp.concatenate([jnp.where(ok, code, 0), jnp.zeros((rows, 128 - length), jnp.int32)], axis=1)
-    low = jnp.take_along_axis(wide0[...], lax.rem(full, 128), axis=1)
-    high = jnp.take_along_axis(wide1[...], lax.rem(full, 128), axis=1)
+    low = jnp.take_along_axis(wide[0], lax.rem(full, 128), axis=1)
+    high = jnp.take_along_axis(wide[1], lax.rem(full, 128), axis=1)
     scores = jnp.where(full < 128, low, high)[:, :length] / TEMP
     scores = jnp.where(ok, scores, -jnp.inf)
     top = jnp.max(scores, axis=1, keepdims=True)
@@ -283,6 +282,7 @@
         rows, length = allowed_ids.shape
         shard_len, width = head_rows.shape
         per = rows * CAP // 128
+        tiles = width // 128
         tbl, hall, meta = pl.pallas_call(
             functools.partial(route_kernel, shard_len, n_model, n_vocab),
             out_shape=(jax.ShapeDtypeStruct((n, per, 128), jnp.int32),
@@ -304,36 +304,37 @@
             compiler_params=pltpu.CompilerParams(collective_id=0, has_side_effects=True),
             name="route",
         )(hidden, allowed_ids, valid_mask, target_pos)
-        chunks = n * rows // GROUP
+        chunks = n * rows * CAP // SLOTS
+        pairs = head_rows.reshape(shard_len // 8, 4, 2, tiles, 128).transpose(0, 3, 1, 2, 4)
         scores = pl.pallas_call(
-            functools.partial(score_kernel, chunks, PIECES),
-            out_shape=jax.ShapeDtypeStruct((chunks, 256), jnp.float32),
+            functools.partial(score_kernel, chunks),
+            out_shape=jax.ShapeDtypeStruct((n, 8, 128), jnp.float32),
             in_specs=[smem, hbm, hbm],
             out_specs=vmem,
             scratch_shapes=[
-                *[pltpu.VMEM((256, width), jnp.bfloat16)] * DEPTH,
-                pltpu.VMEM((chunks, GROUP, width), jnp.bfloat16),
+                *[pltpu.VMEM((SLOTS // 4, tiles, 8, 128), jnp.bfloat16)] * DEPTH,
+                pltpu.VMEM((chunks, SLOTS // CAP, width), jnp.bfloat16),
+                pltpu.VMEM((SLOTS // CAP, width), jnp.float32),
                 pltpu.SemaphoreType.DMA((DEPTH,)),
                 pltpu.SemaphoreType.DMA,
             ],
             compiler_params=pltpu.CompilerParams(vmem_limit_bytes=48 * 1024 * 1024),
             name="score",
-        )(tbl.reshape(n * per, 128), hall.reshape(chunks, GROUP, width), head_rows)
+        )(tbl.reshape(chunks, SLOTS), hall.reshape(chunks, SLOTS // CAP, width), pairs)
         probs, lp = pl.pallas_call(
             functools.partial(finish_kernel, n_model, n_vocab),
             out_shape=(jax.ShapeDtypeStruct((rows, length), jnp.float32), jax.ShapeDtypeStruct((rows,), jnp.float32)),
             in_specs=[vmem, vmem],
             out_specs=(vmem, vmem),
             scratch_shapes=[
-                pltpu.VMEM((n, rows // GROUP, 256), jnp.float32),
-                pltpu.VMEM((rows, 128), jnp.float32),
-                pltpu.VMEM((rows, 128), jnp.float32),
+                pltpu.VMEM((n, 8, 128), jnp.float32),
+                pltpu.VMEM((128, n * 8), jnp.float32),
                 pltpu.SemaphoreType.DMA((n,)),
                 pltpu.SemaphoreType.DMA((n,)),
             ],
             compiler_params=pltpu.CompilerParams(collective_id=1, has_side_effects=True),
             name="finish",
-        )(scores.reshape(n, rows // GROUP, 256), meta)
+        )(scores, meta)
         return probs, lp
 
     return jax.shard_map(local_step, mesh=mesh, in_specs=(row_spec, P(axes, None), row_spec, row_spec, vec_spec),

time: 86.9 us -> 61.3 us (0.71)
  Pallas kernels: 80.3 us -> 54.3 us
    pallas_call x1, Pallas kernels: 53.2 us -> 27.6 us  [local_step(): pl.pallas_call(functools.partial(score_kernel, chunks), out_shape=jax.Sha...]
    unnamed x6 -> x8, local copies, waits for them, and re-layouts: 4.96 us -> 5.48 us
where the time goes in v3:
time: 61.3 us; the launch traced here: 60.4 us
  Pallas kernels  54.3 us (89%)
  local copies, waits for them, and re-layouts  5.48 us (9%)
  between operations  0.67 us (1%)
    pallas_call x1, Pallas kernels, local_step(): pl.pallas_call(functools.partial(score_kernel, chunks), out_shape=jax.Sha...  27.6 us
    pallas_call x1, Pallas kernels, local_step(): pl.pallas_call(functools.partial(route_kernel, shard_len, n_model, n_voca...  20 us
    pallas_call x1, Pallas kernels, local_step(): pl.pallas_call(functools.partial(finish_kernel, n_model, n_vocab), out_sh...  6.66 us
    unnamed x8, local copies, waits for them, and re-layouts  5.48 us

profile of v3, /device:TPU:0, one launch (start us, length us, event | category | flops | bytes accessed | tf_op | source)
XLA Modules:
  0.0 60.4 jit_solution(1040622638513176778)
XLA Ops:
  0.6 20.0 %route.1 = (s32[8,4,128]{2,1,0:T(4,128)}, bf16[8,32,5120]{2,1,0:T(8,128)(2,1)}, s32[32,128]{1,0:T(8,128)}) custom-call(bf16[32,5120]{1,0:T(8,128)(2,1)} %h_ref.1, s32[32,64]{1,0:T(8,128)} %ids_ref.1, s32[32,64]{1,0:T(8,128)} %valid_ref.1, s32[32]{0:T(128)} %tgt_ref.1), custom_call_target="tpu_custom_call" | custom-call | tf_op jit(solution)/shard_map/route/pallas_call | solution.py:286
  20.7 0.0 copy-start
  20.7 1.7 %copy-done = bf16[8,32,5120]{2,1,0:T(8,128)(2,1)S(1)} copy-done((bf16[8,32,5120]{2,1,0:T(8,128)(2,1)S(1)}, bf16[8,32,5120]{2,1,0:T(8,128)(2,1)}, u32[]{:S(2)}) %copy-start) | copy-done | bytes 2621464
  22.4 0.0 copy-start.2
  22.4 0.7 %copy-done.2 = s32[8,4,128]{2,1,0:T(4,128)S(1)} copy-done((s32[8,4,128]{2,1,0:T(4,128)S(1)}, s32[8,4,128]{2,1,0:T(4,128)}, u32[]{:S(2)}) %copy-start.2) | copy-done | bytes 16408
  23.1 27.6 %score.1.sc_ref = f32[8,8,128]{2,1,0:T(8,128)S(1)} custom-call(s32[32,128]{1,0:T(8,128)S(1)} %bitcast.6, bf16[32,8,5120]{2,1,0:T(8,128)(2,1)S(1)} %bitcast.5, bf16[2048,40,4,2,128]{4,3,2,1,0:T(2,128)(2,1)} %bitcast.3.w_hbm), custom_call_target="tpu_custom_call" | custom-call | tf_op jit(solution)/shard_map/score/pallas_call | solution.py:309
  50.7 0.0 copy-start.1
  50.7 0.6 copy-done.1
  51.3 6.7 %finish.1 = (f32[32,64]{1,0:T(8,128)}, f32[32]{0:T(128)}) custom-call(f32[8,8,128]{2,1,0:T(8,128)} %copy-done.1, s32[32,128]{1,0:T(8,128)} %get-tuple-element.7.meta_ref), custom_call_target="tpu_custom_call" | custom-call | tf_op jit(solution)/shard_map/finish/pallas_call | solution.py:324
  58.0 1.3 %copy.9 = f32[32,64]{1,0:T(8,128)} copy(f32[32,64]{1,0:T(8,128)} %get-tuple-element.10) | data formatting | bytes 16384
  59.3 1.1 %copy.10 = f32[32]{0:T(128)} copy(f32[32]{0:T(128)} %get-tuple-element.11) | data formatting | bytes 256
Async XLA Ops:
  20.7 1.7 %copy-start = (bf16[8,32,5120]{2,1,0:T(8,128)(2,1)S(1)}, bf16[8,32,5120]{2,1,0:T(8,128)(2,1)}, u32[]{:S(2)}) copy-start(bf16[8,32,5120]{2,1,0:T(8,128)(2,1)} %get-tuple-element.6) | copy-start | bytes 7864324
  22.4 0.7 %copy-start.2 = (s32[8,4,128]{2,1,0:T(4,128)S(1)}, s32[8,4,128]{2,1,0:T(4,128)}, u32[]{:S(2)}) copy-start(s32[8,4,128]{2,1,0:T(4,128)} %get-tuple-element.5) | copy-start | bytes 49156
  50.7 0.6 %copy-start.1 = (f32[8,8,128]{2,1,0:T(8,128)}, f32[8,8,128]{2,1,0:T(8,128)S(1)}, u32[]{:S(2)}) copy-start(f32[8,8,128]{2,1,0:T(8,128)S(1)} %score.1.sc_ref) | copy-start | bytes 98308

commit v4 on v3

v4 whole, which is shorter than its diff:
```python
import functools

import jax
import jax.numpy as jnp
from jax import lax
from jax.experimental import pallas as pl
from jax.experimental.pallas import tpu as pltpu
from jax.sharding import PartitionSpec as P

MESH = pl.DeviceIdType.MESH
TEMP = 0.5
CAP = 16
SLOTS = 128
DEPTH = 4
STAGES = ((0, 1), (2, 4, 6), (3, 5, 7))


def flip_bits(a, k):
    for bit in (1, 2):
        if k & bit:
            a = a + bit - 2 * bit * lax.rem(lax.div(a, bit), 2)
    return a


def peer(m, v, k, n_vocab):
    return flip_bits(m, k // n_vocab), flip_bits(v, k % n_vocab)


def entry_barrier(n, n_vocab, m, v):
    barrier = pltpu.get_barrier_semaphore()
    for k in range(1, n):
        pm, pv = peer(m, v, k, n_vocab)
        pl.semaphore_signal(barrier, inc=1, device_id={"model": pm, "vocab": pv}, device_id_type=MESH)
    return barrier


def route_kernel(shard_len, n, n_vocab, ids_ref, valid_ref, tgt_ref, tbl_ref, meta_ref, t_ref, send_ref, tin_ref, tsend, trecv):
    rows, length = ids_ref.shape
    m, v = lax.axis_index("model"), lax.axis_index("vocab")
    me = m * n_vocab + v
    barrier = entry_barrier(n, n_vocab, m, v)

    ids = ids_ref[...]
    ok = valid_ref[...] > 0
    owner = jnp.where(ok, lax.div(ids, shard_len), n)
    off = lax.rem(ids, shard_len)
    tri = (lax.broadcasted_iota(jnp.int32, (length, length), 0)
           < lax.broadcasted_iota(jnp.int32, (length, length), 1)).astype(jnp.bfloat16)
    rank = jnp.zeros((rows, length), jnp.float32)
    for s in range(n):
        hit = owner == s
        count = jnp.dot(jnp.where(hit, 1.0, 0.0).astype(jnp.bfloat16), tri, preferred_element_type=jnp.float32)
        rank = rank + jnp.where(hit, count, 0.0)
    rank = rank.astype(jnp.int32)
    slot = jnp.where(ok, owner * CAP + rank, n * CAP)
    pair = off - lax.rem(off, 2)

    lane = lax.broadcasted_iota(jnp.int32, (rows, n * CAP), 1)
    row = lax.broadcasted_iota(jnp.int32, (rows, n * CAP), 0)
    spread = lax.rem(((me * rows + row) * CAP + lax.rem(lane, CAP)) * 4, shard_len)
    table = spread
    for j in range(length):
        table = jnp.where(lane == slot[:, j:j + 1], pair[:, j:j + 1], table)
    t_ref[...] = table

    groups = 128 // CAP
    per = rows // groups
    lane4 = lax.broadcasted_iota(jnp.int32, (per, 128), 1)
    parts = [jnp.zeros((per, 128), jnp.int32) for _ in range(n)]
    for q in range(groups):
        tq = t_ref[pl.ds(q, per, stride=groups), :]
        inside = lax.div(lane4, CAP) == q
        for s in range(n):
            moved = tq if q == s else pltpu.roll(tq, ((q - s) * CAP) % 128, axis=1)
            parts[s] = jnp.where(inside, moved, parts[s])
    for s in range(n):
        send_ref[s] = parts[s]

    code = lax.div(rank, 4) * (n * 8) + owner * 8 + lax.rem(rank, 4) * 2 + lax.rem(off, 2)
    diag = (lax.broadcasted_iota(jnp.int32, (rows, rows), 0) == lax.broadcasted_iota(jnp.int32, (rows, rows), 1))
    tcol = jnp.sum(jnp.where(diag, tgt_ref[...].reshape(1, rows), 0).astype(jnp.float32), axis=1, keepdims=True)
    meta_ref[:, :length] = jnp.where(ok, code, -1)
    meta_ref[:, length:] = jnp.broadcast_to(tcol.astype(jnp.int32), (rows, length))

    pl.semaphore_wait(barrier, n - 1)
    copies = []
    for k in range(1, n):
        pm, pv = peer(m, v, k, n_vocab)
        c = pltpu.make_async_remote_copy(
            src_ref=send_ref.at[pm * n_vocab + pv], dst_ref=tin_ref.at[k], send_sem=tsend.at[k], recv_sem=trecv.at[k],
            device_id={"model": pm, "vocab": pv}, device_id_type=MESH)
        c.start()
        copies.append(c)
    tbl_ref[0] = send_ref[me]
    for k in range(1, n):
        copies[k - 1].wait_recv()
        tbl_ref[k] = tin_ref[k]
    for c in copies:
        c.wait_send()


def score_kernel(blocks, *refs):
    nb = len(blocks)
    tbl_ref, w_hbm, h_refs, out_ref = refs[0], refs[1], refs[2:2 + nb], refs[2 + nb]
    bufs = refs[3 + nb:3 + nb + DEPTH]
    hf_ref, sems = refs[3 + nb + DEPTH:]
    tiles = w_hbm.shape[1]
    nrow = SLOTS // CAP
    quads = CAP // 4
    per = h_refs[0].shape[0] // nrow
    chunks = nb * per

    def table_row(c):
        if isinstance(c, int):
            return blocks[c // per] * per + c % per
        i = lax.div(c, per)
        blk = jnp.int32(blocks[0])
        for z in range(1, nb):
            blk = jnp.where(i == z, blocks[z], blk)
        return blk * per + lax.rem(c, per)

    def issue(r, b, k):
        at = tbl_ref[r, k]
        t, p = lax.shift_right_logical(at, 3), lax.bitwise_and(lax.shift_right_logical(at, 1), 3)
        pltpu.make_async_copy(
            w_hbm.at[t, :, p], bufs[b].at[k // 4, :, pl.ds(2 * (k % 4), 2), :], sems.at[b]).start(priority=k % 2)

    lane = lax.broadcasted_iota(jnp.int32, (8, 128), 1)

    def work(c, b, more):
        ahead = table_row(c + DEPTH - 1) if more else None
        pltpu.make_async_copy(bufs[b], bufs[b], sems.at[b]).wait()
        flat = bufs[b].reshape(SLOTS // 4 * tiles * 8, 128)
        blk, part = lax.div(c, per), lax.rem(c, per)
        for z in range(nb):
            @pl.when(blk == z)
            def _():
                hf_ref[...] = h_refs[z][pl.ds(pl.multiple_of(part * nrow, nrow), nrow), :].astype(jnp.float32)
        got = jnp.zeros((8, 128), jnp.float32)
        base = part * (SLOTS // 4)
        for i in range(nrow):
            acc = [[jnp.zeros((8, 128), jnp.float32)] * 2 for _ in range(quads)]
            for kk in range(0, tiles, 2):
                if more:
                    for k in range(-(-kk * CAP // tiles), -(-(kk + 2) * CAP // tiles)):
                        issue(ahead, (b + DEPTH - 1) % DEPTH, i * CAP + k)
                hb = [jnp.broadcast_to(hf_ref[i:i + 1, (kk + z) * 128:(kk + z + 1) * 128], (8, 128)) for z in (0, 1)]
                for g in range(quads):
                    at = ((i * quads + g) * tiles + kk) * 8
                    x = flat[at:at + 16, :].astype(jnp.float32)
                    acc[g] = [acc[g][0] + x[:8] * hb[0], acc[g][1] + x[8:] * hb[1]]
            for g in range(quads):
                total = jnp.sum(acc[g][0] + acc[g][1], axis=1, keepdims=True)
                got = jnp.where(lane == base + (i * quads + g), total, got)
        fresh = (lane >= base) & (lane < base + SLOTS // 4)
        out_ref[blk] = jnp.where(fresh, got, out_ref[blk])

    for c in range(DEPTH - 1):
        for k in range(SLOTS):
            issue(table_row(c), c, k)

    def step(g, _):
        for b in range(DEPTH):
            work(g * DEPTH + b, b, True)
        return 0

    lax.fori_loop(0, chunks // DEPTH - 1, step, 0)
    for b in range(DEPTH):
        work(jnp.int32(chunks - DEPTH + b), b, b == 0)


def return_kernel(n, n_vocab, *refs):
    ns = len(STAGES)
    scs, out_ref, inb, ssend, srecv = refs[:ns], refs[ns], refs[ns + 1], refs[ns + 2], refs[ns + 3]
    m, v = lax.axis_index("model"), lax.axis_index("vocab")
    me = m * n_vocab + v
    barrier = entry_barrier(n, n_vocab, m, v)
    pl.semaphore_wait(barrier, n - 1)
    copies = []
    for sc, blocks in zip(scs, STAGES):
        for i, k in enumerate(blocks):
            if k == 0:
                out_ref[me] = sc[i]
                continue
            pm, pv = peer(m, v, k, n_vocab)
            c = pltpu.make_async_remote_copy(
                src_ref=sc.at[i], dst_ref=inb.at[k], send_sem=ssend.at[k], recv_sem=srecv.at[k],
                device_id={"model": pm, "vocab": pv}, device_id_type=MESH)
            c.start()
            copies.append((k, c))
    for k, c in copies:
        c.wait_recv()
        pm, pv = peer(m, v, k, n_vocab)
        out_ref[pm * n_vocab + pv] = inb[k]
    for k, c in copies:
        c.wait_send()


def softmax_kernel(sc_ref, meta_ref, p_ref, lp_ref, flip):
    n = sc_ref.shape[0]
    rows, length = p_ref.shape
    flip[...] = sc_ref[...].reshape(n * 8, 128).T
    wide = [jnp.concatenate([flip[pl.ds(q, rows, stride=4), :] for q in (2 * hb, 2 * hb + 1)], axis=1) for hb in (0, 1)]
    meta = meta_ref[...]
    code = meta[:, :length]
    ok = code >= 0
    full = jnp.concatenate([jnp.where(ok, code, 0), jnp.zeros((rows, 128 - length), jnp.int32)], axis=1)
    low = jnp.take_along_axis(wide[0], lax.rem(full, 128), axis=1)
    high = jnp.take_along_axis(wide[1], lax.rem(full, 128), axis=1)
    scores = jnp.where(full < 128, low, high)[:, :length] / TEMP
    scores = jnp.where(ok, scores, -jnp.inf)
    top = jnp.max(scores, axis=1, keepdims=True)
    log_norm = top + jnp.log(jnp.sum(jnp.exp(scores - top), axis=1, keepdims=True))
    p_ref[...] = jnp.where(ok, jnp.exp(scores - log_norm), 0.0)
    at = lax.broadcasted_iota(jnp.int32, (rows, length), 1)
    picked = jnp.sum(jnp.where(at == meta[:, length:], scores, 0.0), axis=1, keepdims=True)
    diag = (lax.broadcasted_iota(jnp.int32, (rows, rows), 0) == lax.broadcasted_iota(jnp.int32, (rows, rows), 1))
    lp_ref[...] = jnp.sum(jnp.where(diag, picked - log_norm, 0.0), axis=0)


def solution(mesh):
    axes = ("model", "vocab")
    n_model, n_vocab = mesh.shape["model"], mesh.shape["vocab"]
    n = n_model * n_vocab
    row_spec = P(("rep",) + axes, None)
    vec_spec = P(("rep",) + axes)
    vmem = pl.BlockSpec(memory_space=pltpu.VMEM)
    hbm = pl.BlockSpec(memory_space=pl.ANY)
    smem = pl.BlockSpec(memory_space=pltpu.SMEM)

    def local_step(hidden, head_rows, allowed_ids, valid_mask, target_pos):
        rows, length = allowed_ids.shape
        shard_len, width = head_rows.shape
        per = rows * CAP // 128
        tiles = width // 128

        def exchange(x, k):
            return lax.ppermute(x, axes, [(s, s ^ k) for s in range(n)])

        blocks = {0: hidden}
        for k in (1, 2, 4, 6):
            blocks[k] = exchange(hidden, k)
        tbl, meta = pl.pallas_call(
            functools.partial(route_kernel, shard_len, n, n_vocab),
            out_shape=(jax.ShapeDtypeStruct((n, per, 128), jnp.int32),
                       jax.ShapeDtypeStruct((rows, 2 * length), jnp.int32)),
            in_specs=[vmem, vmem, vmem],
            out_specs=(vmem, vmem),
            scratch_shapes=[
                pltpu.VMEM((rows, n * CAP), jnp.int32),
                pltpu.VMEM((n, per, 128), jnp.int32),
                pltpu.VMEM((n, per, 128), jnp.int32),
                pltpu.SemaphoreType.DMA((n,)),
                pltpu.SemaphoreType.DMA((n,)),
            ],
            compiler_params=pltpu.CompilerParams(collective_id=0, has_side_effects=True),
            cost_estimate=pl.CostEstimate(flops=10_000_000, bytes_accessed=10_000, transcendentals=0),
            name="route",
        )(allowed_ids, valid_mask, target_pos)
        pairs = head_rows.reshape(shard_len // 8, 4, 2, tiles, 128).transpose(0, 3, 1, 2, 4)
        scores = []
        for stage in STAGES:
            nb = len(stage)
            if len(scores) == 1:
                *far, scores[0] = lax.optimization_barrier((*[blocks[k] for k in (2, 4, 6)], scores[0]))
                for k, x in zip((2, 4, 6), far):
                    blocks[k], blocks[k + 1] = x, exchange(x, 1)
            scores.append(pl.pallas_call(
                functools.partial(score_kernel, stage),
                out_shape=jax.ShapeDtypeStruct((nb, 8, 128), jnp.float32),
                in_specs=[smem, hbm] + [vmem] * nb,
                out_specs=vmem,
                scratch_shapes=[
                    *[pltpu.VMEM((SLOTS // 4, tiles, 8, 128), jnp.bfloat16)] * DEPTH,
                    pltpu.VMEM((SLOTS // CAP, width), jnp.float32),
                    pltpu.SemaphoreType.DMA((DEPTH,)),
                ],
                compiler_params=pltpu.CompilerParams(vmem_limit_bytes=24 * 1024 * 1024),
                cost_estimate=pl.CostEstimate(flops=20_000_000 * nb, bytes_accessed=nb * 10_000_000, transcendentals=0),
                name=f"score{stage[0]}",
            )(tbl.reshape(n * per, 128), pairs, *[blocks[k] for k in stage]))
        back = pl.pallas_call(
            functools.partial(return_kernel, n, n_vocab),
            out_shape=jax.ShapeDtypeStruct((n, 8, 128), jnp.float32),
            in_specs=[vmem] * len(STAGES),
            out_specs=vmem,
            scratch_shapes=[
                pltpu.VMEM((n, 8, 128), jnp.float32),
                pltpu.SemaphoreType.DMA((n,)),
                pltpu.SemaphoreType.DMA((n,)),
            ],
            compiler_params=pltpu.CompilerParams(collective_id=1, has_side_effects=True),
            name="giveback",
        )(*scores)
        return pl.pallas_call(
            softmax_kernel,
            out_shape=(jax.ShapeDtypeStruct((rows, length), jnp.float32), jax.ShapeDtypeStruct((rows,), jnp.float32)),
            in_specs=[vmem, vmem],
            out_specs=(vmem, vmem),
            scratch_shapes=[pltpu.VMEM((128, n * 8), jnp.float32)],
            name="finish",
        )(back, meta)

    return jax.shard_map(local_step, mesh=mesh, in_specs=(row_spec, P(axes, None), row_spec, row_spec, vec_spec),
                         out_specs=(row_spec, vec_spec), check_vma=False)
```

time: 61.3 us -> 67.1 us (1.095)
  starting transfers between devices: 0 us -> 5.51 us
  Pallas kernels: 54.3 us -> 56.7 us
  local copies, waits for them, and re-layouts: 5.48 us -> 3.46 us
    ppermute x0 -> x7, starting transfers between devices: none -> 5.51 us  [exchange(): return lax.ppermute(x, axes, [(s, s ^ k) for s in range(n)])]
    pallas_call x3 -> x6, Pallas kernels: 54.3 us -> 56.7 us  [the longest x3 32.9 us: local_step(): pl.pallas_call(functools.partial(score_kernel, stage), out_shape=jax.Shap...]
    unnamed x8 -> x10, local copies, waits for them, and re-layouts: 5.48 us -> 3.46 us
  transfers between devices with their start and end apart: 0 -> 7, of which waited for: 0 -> 0; matrix products, arithmetic and copies ran while one was open for 0% -> 0% of each run, Pallas kernels for 0% -> 55%
where the time goes in v4:
time: 67.1 us; the launch traced here: 66.4 us
  Pallas kernels  56.7 us (85%)
  starting transfers between devices  5.51 us (8%)
  local copies, waits for them, and re-layouts  3.46 us (5%)
  between operations  0.73 us (1%)
    pallas_call x3, Pallas kernels, local_step(): pl.pallas_call(functools.partial(score_kernel, stage), out_shape=jax.Shap...  32.9 us
    pallas_call x1, Pallas kernels, local_step(): pl.pallas_call(functools.partial(route_kernel, shard_len, n, n_vocab), ou...  15.9 us
    pallas_call x1, Pallas kernels, local_step(): pl.pallas_call(functools.partial(return_kernel, n, n_vocab), out_shape=ja...  6.07 us
    ppermute x7, starting transfers between devices, exchange(): return lax.ppermute(x, axes, [(s, s ^ k) for s in range(n)])  5.51 us
    unnamed x10, local copies, waits for them, and re-layouts  3.46 us
    pallas_call x1, Pallas kernels, local_step(): pl.pallas_call(softmax_kernel, out_shape=(jax.ShapeDtypeStruct((rows, len...  1.79 us
  transfers between devices with their start and end apart: 7, of which 0 were waited for; matrix products, arithmetic and copies ran while one was open for 0% of the time, Pallas kernels for 55%

profile of v4, /device:TPU:0, one launch (start us, length us, event | category | flops | bytes accessed | tf_op | source)
XLA Modules:
  0.0 66.4 jit_solution(5012057097747420654)
XLA Ops:
  0.6 0.9 %collective-permute-start.3 = (bf16[32,5120]{1,0:T(8,128)(2,1)}, bf16[32,5120]{1,0:T(8,128)(2,1)S(1)}, u32[]{:S(2)}, u32[]{:S(2)}) collective-permute-start(bf16[32,5120]{1,0:T(8,128)(2,1)} %refs_2_.1), channel_id=1, source_target_pairs={{0,1},{1,0},{2,3},{3,2},{4,5},{5,4},{6,7},{7,6}} | collective-permute-start | bytes 983048 | tf_op jit(solution)/shard_map/ppermute | solution.py:238
  1.5 3.5 %collective-permute-start.2 = (bf16[32,5120]{1,0:T(8,128)(2,1)}, bf16[32,5120]{1,0:T(8,128)(2,1)S(1)}, u32[]{:S(2)}, u32[]{:S(2)}) collective-permute-start(bf16[32,5120]{1,0:T(8,128)(2,1)} %refs_2_.1), channel_id=1, source_target_pairs={{0,6},{1,7},{2,4},{3,5},{4,2},{5,3},{6,0},{7,1}} | collective-permute-start | bytes 983048 | tf_op jit(solution)/shard_map/ppermute | solution.py:238
  5.0 0.5 collective-permute-start.1
  5.5 0.1 collective-permute-start
  5.6 15.9 %route.1 = (s32[8,4,128]{2,1,0:T(4,128)}, s32[32,128]{1,0:T(8,128)}) custom-call(s32[32,64]{1,0:T(8,128)} %ids_ref.1, s32[32,64]{1,0:T(8,128)} %valid_ref.1, s32[32]{0:T(128)} %tgt_ref.1), custom_call_target="tpu_custom_call" | custom-call | flops 10000000 | bytes 10000 | tf_op jit(solution)/shard_map/route/pallas_call | solution.py:243
  21.5 0.0 collective-permute-done.3.refs_3_
  21.5 0.0 copy-start
  21.5 1.0 %copy-done = bf16[32,5120]{1,0:T(8,128)(2,1)S(1)} copy-done((bf16[32,5120]{1,0:T(8,128)(2,1)S(1)}, bf16[32,5120]{1,0:T(8,128)(2,1)}, u32[]{:S(2)}) %copy-start) | copy-done | bytes 327704
  22.5 0.0 copy-start.1
  22.5 0.7 %copy-done.1 = s32[8,4,128]{2,1,0:T(4,128)S(1)} copy-done((s32[8,4,128]{2,1,0:T(4,128)S(1)}, s32[8,4,128]{2,1,0:T(4,128)}, u32[]{:S(2)}) %copy-start.1) | copy-done | bytes 16408
  23.2 9.0 %score0.1.refs_0_ = f32[2,8,128]{2,1,0:T(8,128)S(1)} custom-call(s32[32,128]{1,0:T(8,128)S(1)} %bitcast.4, bf16[2048,40,4,2,128]{4,3,2,1,0:T(2,128)(2,1)} %bitcast.2.refs_1_, bf16[32,5120]{1,0:T(8,128)(2,1)S(1)} %copy-done, bf16[32,5120]{1,0:T(8,128)(2,1)S(1)} %collective-permute-done.3.refs_3_), custom_call_target="tpu_custom_call" | custom-call | flops 40000000 | bytes 20000000 | tf_op jit(solution)/shard_map/score0/pallas_call | solution.py:268
  32.2 0.0 copy-start.4
  32.2 0.6 copy-done.4
  32.8 0.0 collective-permute-done.2.refs_4_
  32.8 0.0 collective-permute-done.1.refs_3_
  32.8 0.0 collective-permute-done.refs_2_
  32.8 0.0 collective-permute-start.4
  32.9 0.5 collective-permute-start.5
  33.4 0.0 collective-permute-start.6
  33.4 11.6 %score2.1.refs_1_ = f32[3,8,128]{2,1,0:T(8,128)S(1)} custom-call(s32[32,128]{1,0:T(8,128)S(1)} %bitcast.5, bf16[2048,40,4,2,128]{4,3,2,1,0:T(2,128)(2,1)} %bitcast.2.refs_1_, bf16[32,5120]{1,0:T(8,128)(2,1)S(1)} %collective-permute-done.refs_2_, bf16[32,5120]{1,0:T(8,128)(2,1)S(1)} %collective-permute-done.1.refs_3_, ...), custom_call_target="tpu_custom_call" | custom-call | flops 60000000 | bytes 30000000 | tf_op jit(solution)/shard_map/score2/pallas_call | solution.py:268
  45.0 0.0 copy-start.2
  45.1 0.6 copy-done.2
  45.6 0.0 collective-permute-done.4.refs_2_
  45.6 0.0 collective-permute-done.5.refs_3_
  45.7 0.0 collective-permute-done.6.refs_4_
  45.7 12.3 %score3.1.refs_2_ = f32[3,8,128]{2,1,0:T(8,128)S(1)} custom-call(s32[32,128]{1,0:T(8,128)S(1)} %bitcast.6, bf16[2048,40,4,2,128]{4,3,2,1,0:T(2,128)(2,1)} %bitcast.2.refs_1_, bf16[32,5120]{1,0:T(8,128)(2,1)S(1)} %collective-permute-done.4.refs_2_, bf16[32,5120]{1,0:T(8,128)(2,1)S(1)} %collective-permute-done.5.refs_3_, ...), custom_call_target="tpu_custom_call" | custom-call | flops 60000000 | bytes 30000000 | tf_op jit(solution)/shard_map/score3/pallas_call | solution.py:268
  57.9 0.0 copy-start.3
  57.9 0.6 copy-done.3
  58.5 6.1 %giveback.1.sc_ref = f32[8,8,128]{2,1,0:T(8,128)} custom-call(f32[2,8,128]{2,1,0:T(8,128)} %copy-done.4, f32[3,8,128]{2,1,0:T(8,128)} %copy-done.2, f32[3,8,128]{2,1,0:T(8,128)} %copy-done.3), custom_call_target="tpu_custom_call" | custom-call | tf_op jit(solution)/shard_map/giveback/pallas_call | solution.py:282
  64.6 1.8 %finish.1 = (f32[32,64]{1,0:T(8,128)}, f32[32]{0:T(128)}) custom-call(f32[8,8,128]{2,1,0:T(8,128)} %giveback.1.sc_ref, s32[32,128]{1,0:T(8,128)} %get-tuple-element.13.meta_ref), custom_call_target="tpu_custom_call" | custom-call | tf_op jit(solution)/shard_map/finish/pallas_call | solution.py:295
Async XLA Ops:
  0.6 20.9 %collective-permute-start.3 = (bf16[32,5120]{1,0:T(8,128)(2,1)}, bf16[32,5120]{1,0:T(8,128)(2,1)S(1)}, u32[]{:S(2)}, u32[]{:S(2)}) collective-permute-start(bf16[32,5120]{1,0:T(8,128)(2,1)} %refs_2_.1), channel_id=1, source_target_pairs={{0,1},{1,0},{2,3},{3,2},{4,5},{5,4},{6,7},{7,6}} | collective-permute-start | bytes 983048 | tf_op jit(solution)/shard_map/ppermute | solution.py:238
  1.5 31.3 %collective-permute-start.2 = (bf16[32,5120]{1,0:T(8,128)(2,1)}, bf16[32,5120]{1,0:T(8,128)(2,1)S(1)}, u32[]{:S(2)}, u32[]{:S(2)}) collective-permute-start(bf16[32,5120]{1,0:T(8,128)(2,1)} %refs_2_.1), channel_id=1, source_target_pairs={{0,6},{1,7},{2,4},{3,5},{4,2},{5,3},{6,0},{7,1}} | collective-permute-start | bytes 983048 | tf_op jit(solution)/shard_map/ppermute | solution.py:238
  5.0 27.8 %collective-permute-start.1 = (bf16[32,5120]{1,0:T(8,128)(2,1)}, bf16[32,5120]{1,0:T(8,128)(2,1)S(1)}, u32[]{:S(2)}, u32[]{:S(2)}) collective-permute-start(bf16[32,5120]{1,0:T(8,128)(2,1)} %refs_2_.1), channel_id=1, source_target_pairs={{0,4},{1,5},{2,6},{3,7},{4,0},{5,1},{6,2},{7,3}} | collective-permute-start | bytes 983048 | tf_op jit(solution)/shard_map/ppermute | solution.py:238
  5.5 27.3 %collective-permute-start = (bf16[32,5120]{1,0:T(8,128)(2,1)}, bf16[32,5120]{1,0:T(8,128)(2,1)S(1)}, u32[]{:S(2)}, u32[]{:S(2)}) collective-permute-start(bf16[32,5120]{1,0:T(8,128)(2,1)} %refs_2_.1), channel_id=1, source_target_pairs={{0,2},{1,3},{2,0},{3,1},{4,6},{5,7},{6,4},{7,5}} | collective-permute-start | bytes 983048 | tf_op jit(solution)/shard_map/ppermute | solution.py:238
  21.5 1.0 %copy-start = (bf16[32,5120]{1,0:T(8,128)(2,1)S(1)}, bf16[32,5120]{1,0:T(8,128)(2,1)}, u32[]{:S(2)}) copy-start(bf16[32,5120]{1,0:T(8,128)(2,1)} %refs_2_.1) | copy-start | bytes 983044
  22.5 0.7 %copy-start.1 = (s32[8,4,128]{2,1,0:T(4,128)S(1)}, s32[8,4,128]{2,1,0:T(4,128)}, u32[]{:S(2)}) copy-start(s32[8,4,128]{2,1,0:T(4,128)} %get-tuple-element.8) | copy-start | bytes 49156
  32.2 0.6 copy-start.4
  32.8 12.8 %collective-permute-start.4 = (bf16[32,5120]{1,0:T(8,128)(2,1)S(1)}, bf16[32,5120]{1,0:T(8,128)(2,1)S(1)}, u32[]{:S(2)}, u32[]{:S(2)}) collective-permute-start(bf16[32,5120]{1,0:T(8,128)(2,1)S(1)} %collective-permute-done.refs_2_), channel_id=1, source_target_pairs={{0,1},{1,0},{2,3},{3,2},{4,5},{5,4},{6,7},{7,6}} | collective-permute-start | bytes 983048 | tf_op jit(solution)/shard_map/ppermute | solution.py:238
  32.9 12.8 %collective-permute-start.5 = (bf16[32,5120]{1,0:T(8,128)(2,1)S(1)}, bf16[32,5120]{1,0:T(8,128)(2,1)S(1)}, u32[]{:S(2)}, u32[]{:S(2)}) collective-permute-start(bf16[32,5120]{1,0:T(8,128)(2,1)S(1)} %collective-permute-done.1.refs_3_), channel_id=1, source_target_pairs={{0,1},{1,0},{2,3},{3,2},{4,5},{5,4},{6,7},{7,6}} | collective-permute-start | bytes 983048 | tf_op jit(solution)/shard_map/ppermute | solution.py:238
  33.4 12.3 %collective-permute-start.6 = (bf16[32,5120]{1,0:T(8,128)(2,1)S(1)}, bf16[32,5120]{1,0:T(8,128)(2,1)S(1)}, u32[]{:S(2)}, u32[]{:S(2)}) collective-permute-start(bf16[32,5120]{1,0:T(8,128)(2,1)S(1)} %collective-permute-done.2.refs_4_), channel_id=1, source_target_pairs={{0,1},{1,0},{2,3},{3,2},{4,5},{5,4},{6,7},{7,6}} | collective-permute-start | bytes 983048 | tf_op jit(solution)/shard_map/ppermute | solution.py:238
  45.0 0.6 copy-start.2
  57.9 0.6 copy-start.3

commit v5 on v4

--- a/solution.py
+++ b/solution.py
@@ -12,7 +12,7 @@
 CAP = 16
 SLOTS = 128
 DEPTH = 4
-STAGES = ((0, 1), (2, 4, 6), (3, 5, 7))
+STAGES = ((0, 1), (2, 4), (3, 5, 6, 7))
 
 
 def flip_bits(a, k):
@@ -34,7 +34,7 @@
     return barrier
 
 
-def route_kernel(shard_len, n, n_vocab, ids_ref, valid_ref, tgt_ref, tbl_ref, meta_ref, t_ref, send_ref, tin_ref, tsend, trecv):
+def route_kernel(shard_len, n, n_vocab, ids_ref, valid_ref, tgt_ref, h_ref, tbl_ref, meta_ref, h1_ref, hin_ref, t_ref, send_ref, tin_ref, tsend, trecv, hsend, hrecv):
     rows, length = ids_ref.shape
     m, v = lax.axis_index("model"), lax.axis_index("vocab")
     me = m * n_vocab + v
@@ -91,10 +91,18 @@
             device_id={"model": pm, "vocab": pv}, device_id_type=MESH)
         c.start()
         copies.append(c)
+    pm, pv = peer(m, v, 1, n_vocab)
+    hcopy = pltpu.make_async_remote_copy(
+        src_ref=h_ref, dst_ref=hin_ref, send_sem=hsend, recv_sem=hrecv,
+        device_id={"model": pm, "vocab": pv}, device_id_type=MESH)
+    hcopy.start()
     tbl_ref[0] = send_ref[me]
     for k in range(1, n):
         copies[k - 1].wait_recv()
         tbl_ref[k] = tin_ref[k]
+    hcopy.wait_recv()
+    h1_ref[...] = hin_ref[...]
+    hcopy.wait_send()
     for c in copies:
         c.wait_send()
 
@@ -103,7 +111,7 @@
     nb = len(blocks)
     tbl_ref, w_hbm, h_refs, out_ref = refs[0], refs[1], refs[2:2 + nb], refs[2 + nb]
     bufs = refs[3 + nb:3 + nb + DEPTH]
-    hf_ref, sems = refs[3 + nb + DEPTH:]
+    res_ref, hf_ref, sems, osem = refs[3 + nb + DEPTH:]
     tiles = w_hbm.shape[1]
     nrow = SLOTS // CAP
     quads = CAP // 4
@@ -153,7 +161,7 @@
                 total = jnp.sum(acc[g][0] + acc[g][1], axis=1, keepdims=True)
                 got = jnp.where(lane == base + (i * quads + g), total, got)
         fresh = (lane >= base) & (lane < base + SLOTS // 4)
-        out_ref[blk] = jnp.where(fresh, got, out_ref[blk])
+        res_ref[blk] = jnp.where(fresh, got, res_ref[blk])
 
     for c in range(DEPTH - 1):
         for k in range(SLOTS):
@@ -167,6 +175,9 @@
     lax.fori_loop(0, chunks // DEPTH - 1, step, 0)
     for b in range(DEPTH):
         work(jnp.int32(chunks - DEPTH + b), b, b == 0)
+    done = pltpu.make_async_copy(res_ref, out_ref, osem)
+    done.start()
+    done.wait()
 
 
 def return_kernel(n, n_vocab, *refs):
@@ -237,43 +248,50 @@
         def exchange(x, k):
             return lax.ppermute(x, axes, [(s, s ^ k) for s in range(n)])
 
-        blocks = {0: hidden}
-        for k in (1, 2, 4, 6):
-            blocks[k] = exchange(hidden, k)
-        tbl, meta = pl.pallas_call(
+        tbl, meta, beside = pl.pallas_call(
             functools.partial(route_kernel, shard_len, n, n_vocab),
             out_shape=(jax.ShapeDtypeStruct((n, per, 128), jnp.int32),
-                       jax.ShapeDtypeStruct((rows, 2 * length), jnp.int32)),
-            in_specs=[vmem, vmem, vmem],
-            out_specs=(vmem, vmem),
+                       jax.ShapeDtypeStruct((rows, 2 * length), jnp.int32),
+                       jax.ShapeDtypeStruct((rows, width), jnp.bfloat16)),
+            in_specs=[vmem, vmem, vmem, vmem],
+            out_specs=(vmem, vmem, vmem),
             scratch_shapes=[
+                pltpu.VMEM((rows, width), jnp.bfloat16),
                 pltpu.VMEM((rows, n * CAP), jnp.int32),
                 pltpu.VMEM((n, per, 128), jnp.int32),
                 pltpu.VMEM((n, per, 128), jnp.int32),
                 pltpu.SemaphoreType.DMA((n,)),
                 pltpu.SemaphoreType.DMA((n,)),
+                pltpu.SemaphoreType.DMA,
+                pltpu.SemaphoreType.DMA,
             ],
             compiler_params=pltpu.CompilerParams(collective_id=0, has_side_effects=True),
             cost_estimate=pl.CostEstimate(flops=10_000_000, bytes_accessed=10_000, transcendentals=0),
             name="route",
-        )(allowed_ids, valid_mask, target_pos)
+        )(allowed_ids, valid_mask, target_pos, hidden)
+        hidden_after, tbl = lax.optimization_barrier((hidden, tbl))
+        blocks = {0: hidden, 1: beside, **{k: exchange(hidden_after, k) for k in (2, 4, 6)}}
         pairs = head_rows.reshape(shard_len // 8, 4, 2, tiles, 128).transpose(0, 3, 1, 2, 4)
         scores = []
         for stage in STAGES:
             nb = len(stage)
             if len(scores) == 1:
-                *far, scores[0] = lax.optimization_barrier((*[blocks[k] for k in (2, 4, 6)], scores[0]))
-                for k, x in zip((2, 4, 6), far):
-                    blocks[k], blocks[k + 1] = x, exchange(x, 1)
+                blocks[2], blocks[4], scores[0] = lax.optimization_barrier((blocks[2], blocks[4], scores[0]))
+                blocks[3], blocks[5] = exchange(blocks[2], 1), exchange(blocks[4], 1)
+            if len(scores) == 2:
+                blocks[6], scores[1] = lax.optimization_barrier((blocks[6], scores[1]))
+                blocks[7] = exchange(blocks[6], 1)
             scores.append(pl.pallas_call(
                 functools.partial(score_kernel, stage),
                 out_shape=jax.ShapeDtypeStruct((nb, 8, 128), jnp.float32),
                 in_specs=[smem, hbm] + [vmem] * nb,
-                out_specs=vmem,
+                out_specs=pl.BlockSpec(memory_space=pltpu.HBM),
                 scratch_shapes=[
                     *[pltpu.VMEM((SLOTS // 4, tiles, 8, 128), jnp.bfloat16)] * DEPTH,
+                    pltpu.VMEM((nb, 8, 128), jnp.float32),
                     pltpu.VMEM((SLOTS // CAP, width), jnp.float32),
                     pltpu.SemaphoreType.DMA((DEPTH,)),
+                    pltpu.SemaphoreType.DMA,
                 ],
                 compiler_params=pltpu.CompilerParams(vmem_limit_bytes=24 * 1024 * 1024),
                 cost_estimate=pl.CostEstimate(flops=20_000_000 * nb, bytes_accessed=nb * 10_000_000, transcendentals=0),

time: 67.1 us -> 62.8 us (0.936)
  Pallas kernels: 56.7 us -> 49.3 us
  waiting for transfers between devices: 0.02 us -> 3.55 us
  starting transfers between devices: 5.51 us -> 4.09 us
  local copies, waits for them, and re-layouts: 3.46 us -> 4.44 us
    pallas_call x1, Pallas kernels: 15.9 us -> 8.85 us  [local_step(): pl.pallas_call(functools.partial(route_kernel, shard_len, n, n_vocab), ou...]
    ppermute x7 -> x6, waiting for transfers between devices: 0.02 us -> 3.55 us  [exchange(): return lax.ppermute(x, axes, [(s, s ^ k) for s in range(n)])]
    ppermute x7 -> x6, starting transfers between devices: 5.51 us -> 4.09 us  [exchange(): return lax.ppermute(x, axes, [(s, s ^ k) for s in range(n)])]
    unnamed x10 -> x14, local copies, waits for them, and re-layouts: 3.46 us -> 4.44 us
  transfers between devices with their start and end apart: 7 -> 6, of which waited for: 0 -> 2; matrix products, arithmetic and copies ran while one was open for 0% -> 0% of each run, Pallas kernels for 55% -> 28%
where the time goes in v5:
time: 62.8 us; the launch traced here: 62.1 us
  Pallas kernels  49.3 us (79%)
  local copies, waits for them, and re-layouts  4.44 us (7%)
  starting transfers between devices  4.09 us (7%)
  waiting for transfers between devices  3.55 us (6%)
  between operations  0.71 us (1%)
    pallas_call x3, Pallas kernels, local_step(): pl.pallas_call(functools.partial(score_kernel, stage), out_shape=jax.Shap...  32.6 us
    pallas_call x1, Pallas kernels, local_step(): pl.pallas_call(functools.partial(route_kernel, shard_len, n, n_vocab), ou...  8.85 us
    pallas_call x1, Pallas kernels, local_step(): pl.pallas_call(functools.partial(return_kernel, n, n_vocab), out_shape=ja...  6.11 us
    unnamed x14, local copies, waits for them, and re-layouts  4.44 us
    ppermute x6, starting transfers between devices, exchange(): return lax.ppermute(x, axes, [(s, s ^ k) for s in range(n)])  4.09 us
    ppermute x6, waiting for transfers between devices, exchange(): return lax.ppermute(x, axes, [(s, s ^ k) for s in range(n)])  3.55 us
    pallas_call x1, Pallas kernels, local_step(): pl.pallas_call(softmax_kernel, out_shape=(jax.ShapeDtypeStruct((rows, len...  1.79 us
  transfers between devices with their start and end apart: 6, of which 2 were waited for; matrix products, arithmetic and copies ran while one was open for 0% of the time, Pallas kernels for 28%

profile of v5, /device:TPU:0, one launch (start us, length us, event | category | flops | bytes accessed | tf_op | source)
XLA Modules:
  0.0 62.1 jit_solution(14192165495955222884)
XLA Ops:
  0.6 8.8 %route.1 = (s32[8,4,128]{2,1,0:T(4,128)}, s32[32,128]{1,0:T(8,128)}, bf16[32,5120]{1,0:T(8,128)(2,1)}) custom-call(s32[32,64]{1,0:T(8,128)} %ids_ref.1, s32[32,64]{1,0:T(8,128)} %valid_ref.1, s32[32]{0:T(128)} %tgt_ref.1, bf16[32,5120]{1,0:T(8,128)(2,1)} %refs_2_.1), custom_call_target="tpu_custom_call" | custom-call | flops 10000000 | bytes 10000 | tf_op jit(solution)/shard_map/route/pallas_call | solution.py:251
  9.5 1.1 %collective-permute-start = (bf16[32,5120]{1,0:T(8,128)(2,1)}, bf16[32,5120]{1,0:T(8,128)(2,1)S(1)}, u32[]{:S(2)}, u32[]{:S(2)}) collective-permute-start(bf16[32,5120]{1,0:T(8,128)(2,1)} %refs_2_.1), channel_id=1, source_target_pairs={{0,2},{1,3},{2,0},{3,1},{4,6},{5,7},{6,4},{7,5}} | collective-permute-start | bytes 983048 | tf_op jit(solution)/shard_map/ppermute | solution.py:249
  10.5 1.5 %collective-permute-start.1 = (bf16[32,5120]{1,0:T(8,128)(2,1)}, bf16[32,5120]{1,0:T(8,128)(2,1)S(1)}, u32[]{:S(2)}, u32[]{:S(2)}) collective-permute-start(bf16[32,5120]{1,0:T(8,128)(2,1)} %refs_2_.1), channel_id=1, source_target_pairs={{0,4},{1,5},{2,6},{3,7},{4,0},{5,1},{6,2},{7,3}} | collective-permute-start | bytes 983048 | tf_op jit(solution)/shard_map/ppermute | solution.py:249
  12.0 1.0 %collective-permute-start.2 = (bf16[32,5120]{1,0:T(8,128)(2,1)}, bf16[32,5120]{1,0:T(8,128)(2,1)S(1)}, u32[]{:S(2)}, u32[]{:S(2)}) collective-permute-start(bf16[32,5120]{1,0:T(8,128)(2,1)} %refs_2_.1), channel_id=1, source_target_pairs={{0,6},{1,7},{2,4},{3,5},{4,2},{5,3},{6,0},{7,1}} | collective-permute-start | bytes 983048 | tf_op jit(solution)/shard_map/ppermute | solution.py:249
  13.0 0.0 copy-start
  13.0 1.0 %copy-done = bf16[32,5120]{1,0:T(8,128)(2,1)S(1)} copy-done((bf16[32,5120]{1,0:T(8,128)(2,1)S(1)}, bf16[32,5120]{1,0:T(8,128)(2,1)}, u32[]{:S(2)}) %copy-start) | copy-done | bytes 327704
  14.0 0.0 copy-start.1
  14.0 1.0 %copy-done.1 = bf16[32,5120]{1,0:T(8,128)(2,1)S(1)} copy-done((bf16[32,5120]{1,0:T(8,128)(2,1)S(1)}, bf16[32,5120]{1,0:T(8,128)(2,1)}, u32[]{:S(2)}) %copy-start.1) | copy-done | bytes 327704
  14.9 0.0 copy-start.2
  14.9 0.7 %copy-done.2 = s32[8,4,128]{2,1,0:T(4,128)S(1)} copy-done((s32[8,4,128]{2,1,0:T(4,128)S(1)}, s32[8,4,128]{2,1,0:T(4,128)}, u32[]{:S(2)}) %copy-start.2) | copy-done | bytes 16408
  15.7 0.0 copy-start.3
  15.7 8.8 %score0.1.refs_0_ = f32[2,8,128]{2,1,0:T(8,128)S(1)} custom-call(s32[32,128]{1,0:T(8,128)S(1)} %bitcast.4, bf16[2048,40,4,2,128]{4,3,2,1,0:T(2,128)(2,1)} %bitcast.2.refs_1_, bf16[32,5120]{1,0:T(8,128)(2,1)S(1)} %copy-done, bf16[32,5120]{1,0:T(8,128)(2,1)S(1)} %copy-done.1), custom_call_target="tpu_custom_call" | custom-call | flops 40000000 | bytes 20000000 | tf_op jit(solution)/shard_map/score0/pallas_call | solution.py:284
  24.5 0.0 copy-start.5
  24.5 0.6 copy-done.5
  25.1 0.0 collective-permute-done.refs_2_
  25.1 2.0 %collective-permute-done.1.refs_3_ = bf16[32,5120]{1,0:T(8,128)(2,1)S(1)} collective-permute-done((bf16[32,5120]{1,0:T(8,128)(2,1)}, bf16[32,5120]{1,0:T(8,128)(2,1)S(1)}, u32[]{:S(2)}, u32[]{:S(2)}) %collective-permute-start.1) | collective-permute-done | bytes 327712 | tf_op jit(solution)/shard_map/ppermute | solution.py:249
  27.0 0.0 collective-permute-start.3
  27.0 0.5 collective-permute-start.4
  27.6 0.0 copy-done.3
  27.6 8.6 %score2.1.refs_1_ = f32[2,8,128]{2,1,0:T(8,128)S(1)} custom-call(s32[32,128]{1,0:T(8,128)S(1)} %bitcast.5, bf16[2048,40,4,2,128]{4,3,2,1,0:T(2,128)(2,1)} %bitcast.2.refs_1_, bf16[32,5120]{1,0:T(8,128)(2,1)S(1)} %collective-permute-done.refs_2_, bf16[32,5120]{1,0:T(8,128)(2,1)S(1)} %collective-permute-done.1.refs_3_), custom_call_target="tpu_custom_call" | custom-call | flops 40000000 | bytes 20000000 | tf_op jit(solution)/shard_map/score2/pallas_call | solution.py:284
  36.2 0.0 copy-start.6
  36.2 0.6 copy-done.6
  36.8 0.0 collective-permute-done.2.refs_4_
  36.8 0.1 collective-permute-start.5
  36.8 0.0 collective-permute-done.3.refs_2_
  36.8 0.0 collective-permute-done.4.refs_3_
  36.8 1.6 %collective-permute-done.5.refs_5_ = bf16[32,5120]{1,0:T(8,128)(2,1)S(1)} collective-permute-done((bf16[32,5120]{1,0:T(8,128)(2,1)S(1)}, bf16[32,5120]{1,0:T(8,128)(2,1)S(1)}, u32[]{:S(2)}, u32[]{:S(2)}) %collective-permute-start.5) | collective-permute-done | bytes 327712 | tf_op jit(solution)/shard_map/ppermute | solution.py:249
  38.4 15.2 %score3.1.refs_2_ = f32[4,8,128]{2,1,0:T(8,128)S(1)} custom-call(s32[32,128]{1,0:T(8,128)S(1)} %bitcast.6, bf16[2048,40,4,2,128]{4,3,2,1,0:T(2,128)(2,1)} %bitcast.2.refs_1_, bf16[32,5120]{1,0:T(8,128)(2,1)S(1)} %collective-permute-done.3.refs_2_, bf16[32,5120]{1,0:T(8,128)(2,1)S(1)} %collective-permute-done.4.refs_3_, ...), custom_call_target="tpu_custom_call" | custom-call | flops 80000000 | bytes 40000000 | tf_op jit(solution)/shard_map/score3/pallas_call | solution.py:284
  53.6 0.0 copy-start.4
  53.6 0.6 copy-done.4
  54.2 6.1 %giveback.1.sc_ref = f32[8,8,128]{2,1,0:T(8,128)} custom-call(f32[2,8,128]{2,1,0:T(8,128)} %copy-done.5, f32[2,8,128]{2,1,0:T(8,128)} %copy-done.6, f32[4,8,128]{2,1,0:T(8,128)} %copy-done.4), custom_call_target="tpu_custom_call" | custom-call | tf_op jit(solution)/shard_map/giveback/pallas_call | solution.py:300
  60.3 1.8 %finish.1 = (f32[32,64]{1,0:T(8,128)}, f32[32]{0:T(128)}) custom-call(f32[8,8,128]{2,1,0:T(8,128)} %giveback.1.sc_ref, s32[32,128]{1,0:T(8,128)} %get-tuple-element.21.meta_ref), custom_call_target="tpu_custom_call" | custom-call | tf_op jit(solution)/shard_map/finish/pallas_call | solution.py:313
Async XLA Ops:
  9.5 15.6 %collective-permute-start = (bf16[32,5120]{1,0:T(8,128)(2,1)}, bf16[32,5120]{1,0:T(8,128)(2,1)S(1)}, u32[]{:S(2)}, u32[]{:S(2)}) collective-permute-start(bf16[32,5120]{1,0:T(8,128)(2,1)} %refs_2_.1), channel_id=1, source_target_pairs={{0,2},{1,3},{2,0},{3,1},{4,6},{5,7},{6,4},{7,5}} | collective-permute-start | bytes 983048 | tf_op jit(solution)/shard_map/ppermute | solution.py:249
  10.5 16.5 %collective-permute-start.1 = (bf16[32,5120]{1,0:T(8,128)(2,1)}, bf16[32,5120]{1,0:T(8,128)(2,1)S(1)}, u32[]{:S(2)}, u32[]{:S(2)}) collective-permute-start(bf16[32,5120]{1,0:T(8,128)(2,1)} %refs_2_.1), channel_id=1, source_target_pairs={{0,4},{1,5},{2,6},{3,7},{4,0},{5,1},{6,2},{7,3}} | collective-permute-start | bytes 983048 | tf_op jit(solution)/shard_map/ppermute | solution.py:249
  12.0 24.7 %collective-permute-start.2 = (bf16[32,5120]{1,0:T(8,128)(2,1)}, bf16[32,5120]{1,0:T(8,128)(2,1)S(1)}, u32[]{:S(2)}, u32[]{:S(2)}) collective-permute-start(bf16[32,5120]{1,0:T(8,128)(2,1)} %refs_2_.1), channel_id=1, source_target_pairs={{0,6},{1,7},{2,4},{3,5},{4,2},{5,3},{6,0},{7,1}} | collective-permute-start | bytes 983048 | tf_op jit(solution)/shard_map/ppermute | solution.py:249
  13.0 1.0 %copy-start = (bf16[32,5120]{1,0:T(8,128)(2,1)S(1)}, bf16[32,5120]{1,0:T(8,128)(2,1)}, u32[]{:S(2)}) copy-start(bf16[32,5120]{1,0:T(8,128)(2,1)} %refs_2_.1) | copy-start | bytes 983044
  14.0 1.0 %copy-start.1 = (bf16[32,5120]{1,0:T(8,128)(2,1)S(1)}, bf16[32,5120]{1,0:T(8,128)(2,1)}, u32[]{:S(2)}) copy-start(bf16[32,5120]{1,0:T(8,128)(2,1)} %get-tuple-element.15.refs_3_) | copy-start | bytes 983044
  14.9 0.7 %copy-start.2 = (s32[8,4,128]{2,1,0:T(4,128)S(1)}, s32[8,4,128]{2,1,0:T(4,128)}, u32[]{:S(2)}) copy-start(s32[8,4,128]{2,1,0:T(4,128)} %get-tuple-element.14) | copy-start | bytes 49156
  15.7 11.9 %copy-start.3 = (s32[8,4,128]{2,1,0:T(4,128)S(1)}, s32[8,4,128]{2,1,0:T(4,128)}, u32[]{:S(2)}) copy-start(s32[8,4,128]{2,1,0:T(4,128)} %get-tuple-element.14) | copy-start | bytes 49156
  24.5 0.6 copy-start.5
  27.0 9.8 %collective-permute-start.3 = (bf16[32,5120]{1,0:T(8,128)(2,1)S(1)}, bf16[32,5120]{1,0:T(8,128)(2,1)S(1)}, u32[]{:S(2)}, u32[]{:S(2)}) collective-permute-start(bf16[32,5120]{1,0:T(8,128)(2,1)S(1)} %collective-permute-done.refs_2_), channel_id=1, source_target_pairs={{0,1},{1,0},{2,3},{3,2},{4,5},{5,4},{6,7},{7,6}} | collective-permute-start | bytes 983048 | tf_op jit(solution)/shard_map/ppermute | solution.py:249
  27.0 9.8 %collective-permute-start.4 = (bf16[32,5120]{1,0:T(8,128)(2,1)S(1)}, bf16[32,5120]{1,0:T(8,128)(2,1)S(1)}, u32[]{:S(2)}, u32[]{:S(2)}) collective-permute-start(bf16[32,5120]{1,0:T(8,128)(2,1)S(1)} %collective-permute-done.1.refs_3_), channel_id=1, source_target_pairs={{0,1},{1,0},{2,3},{3,2},{4,5},{5,4},{6,7},{7,6}} | collective-permute-start | bytes 983048 | tf_op jit(solution)/shard_map/ppermute | solution.py:249
  36.2 0.6 copy-start.6
  36.8 1.6 %collective-permute-start.5 = (bf16[32,5120]{1,0:T(8,128)(2,1)S(1)}, bf16[32,5120]{1,0:T(8,128)(2,1)S(1)}, u32[]{:S(2)}, u32[]{:S(2)}) collective-permute-start(bf16[32,5120]{1,0:T(8,128)(2,1)S(1)} %collective-permute-done.2.refs_4_), channel_id=1, source_target_pairs={{0,1},{1,0},{2,3},{3,2},{4,5},{5,4},{6,7},{7,6}} | collective-permute-start | bytes 983048 | tf_op jit(solution)/shard_map/ppermute | solution.py:249
  53.6 0.6 copy-start.4

commit v6 on v4

--- a/solution.py
+++ b/solution.py
@@ -12,7 +12,6 @@
 CAP = 16
 SLOTS = 128
 DEPTH = 4
-STAGES = ((0, 1), (2, 4, 6), (3, 5, 7))
 
 
 def flip_bits(a, k):
@@ -34,11 +33,50 @@
     return barrier
 
 
-def route_kernel(shard_len, n, n_vocab, ids_ref, valid_ref, tgt_ref, tbl_ref, meta_ref, t_ref, send_ref, tin_ref, tsend, trecv):
+def route_kernel(shard_len, n, n_vocab, ids_hbm, valid_hbm, tgt_hbm, h_hbm, tbl_out, meta_out, hall_out,
+                 ids_ref, valid_ref, tgt_ref, meta_ref, t_ref, send_ref, tin_ref, hbuf, tsend, trecv, hsend, hrecv, lsem, osem):
     rows, length = ids_ref.shape
     m, v = lax.axis_index("model"), lax.axis_index("vocab")
     me = m * n_vocab + v
     barrier = entry_barrier(n, n_vocab, m, v)
+    loads = [pltpu.make_async_copy(src, dst, lsem.at[i]) for i, (src, dst) in enumerate(
+        ((h_hbm, hbuf.at[0]), (ids_hbm, ids_ref), (valid_hbm, valid_ref), (tgt_hbm, tgt_ref)))]
+    for c in loads:
+        c.start()
+
+    half = rows // 2
+    lo, hi, every = pl.ds(0, half), pl.ds(half, half), pl.ds(0, rows)
+    sends = []
+
+    def send(src, dst, part, to):
+        pm, pv = peer(m, v, to, n_vocab)
+        i = len(sends)
+        sends.append(pltpu.make_async_remote_copy(
+            src_ref=hbuf.at[src, part], dst_ref=hbuf.at[dst, part], send_sem=hsend.at[i], recv_sem=hrecv.at[i],
+            device_id={"model": pm, "vocab": pv}, device_id_type=MESH))
+        return sends[-1]
+
+    own_x = [send(0, 2, lo, 2), send(0, 2, hi, 2)]
+    own_y = [send(0, 4, lo, 4), send(0, 4, hi, 4)]
+    own_p = send(0, 1, every, 1)
+    x_to_y, y_to_x = send(2, 6, lo, 4), send(4, 6, hi, 2)
+    x_p = [send(2, 3, lo, 1), send(2, 3, hi, 1)]
+    y_p = [send(4, 5, lo, 1), send(4, 5, hi, 1)]
+    d_p = [send(6, 7, lo, 1), send(6, 7, hi, 1)]
+
+    loads[0].wait()
+    pl.semaphore_wait(barrier, n - 1)
+    for c in (own_x[0], own_y[1], own_p, own_x[1], own_y[0]):
+        c.start()
+    outs = []
+
+    def keep(src, dst):
+        outs.append(pltpu.make_async_copy(src, dst, osem.at[len(outs)]))
+        outs[-1].start()
+
+    keep(hbuf.at[0], hall_out.at[0])
+    for c in loads[1:]:
+        c.wait()
 
     ids = ids_ref[...]
     ok = valid_ref[...] > 0
@@ -82,7 +120,7 @@
     meta_ref[:, :length] = jnp.where(ok, code, -1)
     meta_ref[:, length:] = jnp.broadcast_to(tcol.astype(jnp.int32), (rows, length))
 
-    pl.semaphore_wait(barrier, n - 1)
+    tin_ref[0] = send_ref[me]
     copies = []
     for k in range(1, n):
         pm, pv = peer(m, v, k, n_vocab)
@@ -91,33 +129,55 @@
             device_id={"model": pm, "vocab": pv}, device_id_type=MESH)
         c.start()
         copies.append(c)
-    tbl_ref[0] = send_ref[me]
-    for k in range(1, n):
-        copies[k - 1].wait_recv()
-        tbl_ref[k] = tin_ref[k]
+
+    own_x[0].wait_recv()
+    x_to_y.start()
+    x_p[0].start()
+    own_y[1].wait_recv()
+    y_to_x.start()
+    y_p[1].start()
+    keep(meta_ref, meta_out)
+    own_p.wait_recv()
+    keep(hbuf.at[1], hall_out.at[1])
+    own_x[1].wait_recv()
+    x_p[1].start()
+    keep(hbuf.at[2], hall_out.at[2])
+    own_y[0].wait_recv()
+    y_p[0].start()
+    keep(hbuf.at[4], hall_out.at[4])
     for c in copies:
+        c.wait_recv()
+    keep(tin_ref, tbl_out)
+    for c in x_p:
+        c.wait_recv()
+    keep(hbuf.at[3], hall_out.at[3])
+    for c in y_p:
+        c.wait_recv()
+    keep(hbuf.at[5], hall_out.at[5])
+    x_to_y.wait_recv()
+    d_p[0].start()
+    keep(hbuf.at[6, lo], hall_out.at[6, lo])
+    y_to_x.wait_recv()
+    d_p[1].start()
+    keep(hbuf.at[6, hi], hall_out.at[6, hi])
+    d_p[0].wait_recv()
+    keep(hbuf.at[7, lo], hall_out.at[7, lo])
+    d_p[1].wait_recv()
+    keep(hbuf.at[7, hi], hall_out.at[7, hi])
+    for c in sends + copies:
         c.wait_send()
-
-
-def score_kernel(blocks, *refs):
-    nb = len(blocks)
-    tbl_ref, w_hbm, h_refs, out_ref = refs[0], refs[1], refs[2:2 + nb], refs[2 + nb]
-    bufs = refs[3 + nb:3 + nb + DEPTH]
-    hf_ref, sems = refs[3 + nb + DEPTH:]
+    for c in outs:
+        c.wait()
+
+
+def score_kernel(tbl_ref, w_hbm, h_hbm, out_ref, *scratch):
+    bufs = scratch[:DEPTH]
+    h_ref, hf_ref, sems, hsem = scratch[DEPTH:]
     tiles = w_hbm.shape[1]
     nrow = SLOTS // CAP
     quads = CAP // 4
-    per = h_refs[0].shape[0] // nrow
-    chunks = nb * per
-
-    def table_row(c):
-        if isinstance(c, int):
-            return blocks[c // per] * per + c % per
-        i = lax.div(c, per)
-        blk = jnp.int32(blocks[0])
-        for z in range(1, nb):
-            blk = jnp.where(i == z, blocks[z], blk)
-        return blk * per + lax.rem(c, per)
+    chunks = tbl_ref.shape[0]
+    per = chunks // out_ref.shape[0]
 
     def issue(r, b, k):
         at = tbl_ref[r, k]
@@ -128,14 +188,11 @@
     lane = lax.broadcasted_iota(jnp.int32, (8, 128), 1)
 
     def work(c, b, more):
-        ahead = table_row(c + DEPTH - 1) if more else None
+        ahead = c + DEPTH - 1
         pltpu.make_async_copy(bufs[b], bufs[b], sems.at[b]).wait()
         flat = bufs[b].reshape(SLOTS // 4 * tiles * 8, 128)
         blk, part = lax.div(c, per), lax.rem(c, per)
-        for z in range(nb):
-            @pl.when(blk == z)
-            def _():
-                hf_ref[...] = h_refs[z][pl.ds(pl.multiple_of(part * nrow, nrow), nrow), :].astype(jnp.float32)
+        hf_ref[...] = h_ref[c].astype(jnp.float32)
         got = jnp.zeros((8, 128), jnp.float32)
         base = part * (SLOTS // 4)
         for i in range(nrow):
@@ -155,9 +212,14 @@
         fresh = (lane >= base) & (lane < base + SLOTS // 4)
         out_ref[blk] = jnp.where(fresh, got, out_ref[blk])
 
-    for c in range(DEPTH - 1):
+    for k in range(SLOTS):
+        issue(0, 0, k)
+    hcopy = pltpu.make_async_copy(h_hbm, h_ref, hsem)
+    hcopy.start()
+    for c in range(1, DEPTH - 1):
         for k in range(SLOTS):
-            issue(table_row(c), c, k)
+            issue(c, c, k)
+    hcopy.wait()
 
     def step(g, _):
         for b in range(DEPTH):
@@ -169,31 +231,29 @@
         work(jnp.int32(chunks - DEPTH + b), b, b == 0)
 
 
-def return_kernel(n, n_vocab, *refs):
-    ns = len(STAGES)
-    scs, out_ref, inb, ssend, srecv = refs[:ns], refs[ns], refs[ns + 1], refs[ns + 2], refs[ns + 3]
+def return_kernel(n, n_vocab, sc_hbm, out_hbm, sc_ref, lsem, ssend, srecv):
     m, v = lax.axis_index("model"), lax.axis_index("vocab")
     me = m * n_vocab + v
     barrier = entry_barrier(n, n_vocab, m, v)
+    load = pltpu.make_async_copy(sc_hbm, sc_ref, lsem.at[0])
+    load.start()
+    load.wait()
     pl.semaphore_wait(barrier, n - 1)
     copies = []
-    for sc, blocks in zip(scs, STAGES):
-        for i, k in enumerate(blocks):
-            if k == 0:
-                out_ref[me] = sc[i]
-                continue
-            pm, pv = peer(m, v, k, n_vocab)
-            c = pltpu.make_async_remote_copy(
-                src_ref=sc.at[i], dst_ref=inb.at[k], send_sem=ssend.at[k], recv_sem=srecv.at[k],
-                device_id={"model": pm, "vocab": pv}, device_id_type=MESH)
-            c.start()
-            copies.append((k, c))
-    for k, c in copies:
+    for k in range(1, n):
+        pm, pv = peer(m, v, k, n_vocab)
+        c = pltpu.make_async_remote_copy(
+            src_ref=sc_ref.at[k], dst_ref=out_hbm.at[me], send_sem=ssend.at[k], recv_sem=srecv.at[k],
+            device_id={"model": pm, "vocab": pv}, device_id_type=MESH)
+        c.start()
+        copies.append(c)
+    own = pltpu.make_async_copy(sc_ref.at[0], out_hbm.at[me], lsem.at[1])
+    own.start()
+    for c in copies:
         c.wait_recv()
-        pm, pv = peer(m, v, k, n_vocab)
-        out_ref[pm * n_vocab + pv] = inb[k]
-    for k, c in copies:
+    for c in copies:
         c.wait_send()
+    own.wait()
 
 
 def softmax_kernel(sc_ref, meta_ref, p_ref, lp_ref, flip):
@@ -234,64 +294,63 @@
         per = rows * CAP // 128
         tiles = width // 128
 
-        def exchange(x, k):
-            return lax.ppermute(x, axes, [(s, s ^ k) for s in range(n)])
-
-        blocks = {0: hidden}
-        for k in (1, 2, 4, 6):
-            blocks[k] = exchange(hidden, k)
-        tbl, meta = pl.pallas_call(
+        chunks = n * rows * CAP // SLOTS
+        tbl, meta, hall = pl.pallas_call(
             functools.partial(route_kernel, shard_len, n, n_vocab),
             out_shape=(jax.ShapeDtypeStruct((n, per, 128), jnp.int32),
-                       jax.ShapeDtypeStruct((rows, 2 * length), jnp.int32)),
-            in_specs=[vmem, vmem, vmem],
-            out_specs=(vmem, vmem),
+                       jax.ShapeDtypeStruct((rows, 2 * length), jnp.int32),
+                       jax.ShapeDtypeStruct((n, rows, width), jnp.bfloat16)),
+            in_specs=[hbm] * 4,
+            out_specs=(hbm, hbm, hbm),
             scratch_shapes=[
+                pltpu.VMEM((rows, length), jnp.int32),
+                pltpu.VMEM((rows, length), jnp.int32),
+                pltpu.VMEM((rows,), jnp.int32),
+                pltpu.VMEM((rows, 2 * length), jnp.int32),
                 pltpu.VMEM((rows, n * CAP), jnp.int32),
                 pltpu.VMEM((n, per, 128), jnp.int32),
                 pltpu.VMEM((n, per, 128), jnp.int32),
+                pltpu.VMEM((n, rows, width), jnp.bfloat16),
                 pltpu.SemaphoreType.DMA((n,)),
                 pltpu.SemaphoreType.DMA((n,)),
+                pltpu.SemaphoreType.DMA((13,)),
+                pltpu.SemaphoreType.DMA((13,)),
+                pltpu.SemaphoreType.DMA((4,)),
+                pltpu.SemaphoreType.DMA((12,)),
             ],
             compiler_params=pltpu.CompilerParams(collective_id=0, has_side_effects=True),
-            cost_estimate=pl.CostEstimate(flops=10_000_000, bytes_accessed=10_000, transcendentals=0),
             name="route",
-        )(allowed_ids, valid_mask, target_pos)
+        )(allowed_ids, valid_mask, target_pos, hidden)
         pairs = head_rows.reshape(shard_len // 8, 4, 2, tiles, 128).transpose(0, 3, 1, 2, 4)
-        scores = []
-        for stage in STAGES:
-            nb = len(stage)
-            if len(scores) == 1:
-                *far, scores[0] = lax.optimization_barrier((*[blocks[k] for k in (2, 4, 6)], scores[0]))
-                for k, x in zip((2, 4, 6), far):
-                    blocks[k], blocks[k + 1] = x, exchange(x, 1)
-            scores.append(pl.pallas_call(
-                functools.partial(score_kernel, stage),
-                out_shape=jax.ShapeDtypeStruct((nb, 8, 128), jnp.float32),
-                in_specs=[smem, hbm] + [vmem] * nb,
-                out_specs=vmem,
-                scratch_shapes=[
-                    *[pltpu.VMEM((SLOTS // 4, tiles, 8, 128), jnp.bfloat16)] * DEPTH,
-                    pltpu.VMEM((SLOTS // CAP, width), jnp.float32),
-                    pltpu.SemaphoreType.DMA((DEPTH,)),
-                ],
-                compiler_params=pltpu.CompilerParams(vmem_limit_bytes=24 * 1024 * 1024),
-                cost_estimate=pl.CostEstimate(flops=20_000_000 * nb, bytes_accessed=nb * 10_000_000, transcendentals=0),
-                name=f"score{stage[0]}",
-            )(tbl.reshape(n * per, 128), pairs, *[blocks[k] for k in stage]))
+        scores = pl.pallas_call(
+            score_kernel,
+            out_shape=jax.ShapeDtypeStruct((n, 8, 128), jnp.float32),
+            in_specs=[smem, hbm, hbm],
+            out_specs=vmem,
+            scratch_shapes=[
+                *[pltpu.VMEM((SLOTS // 4, tiles, 8, 128), jnp.bfloat16)] * DEPTH,
+                pltpu.VMEM((chunks, SLOTS // CAP, width), jnp.bfloat16),
+                pltpu.VMEM((SLOTS // CAP, width), jnp.float32),
+                pltpu.SemaphoreType.DMA((DEPTH,)),
+                pltpu.SemaphoreType.DMA,
+            ],
+            compiler_params=pltpu.CompilerParams(vmem_limit_bytes=67_000_000),
+            name="score",
+        )(tbl.reshape(n * per, 128), pairs, hall.reshape(chunks, SLOTS // CAP, width))
         back = pl.pallas_call(
             functools.partial(return_kernel, n, n_vocab),
             out_shape=jax.ShapeDtypeStruct((n, 8, 128), jnp.float32),
-            in_specs=[vmem] * len(STAGES),
-            out_specs=vmem,
+            in_specs=[hbm],
+            out_specs=hbm,
             scratch_shapes=[
                 pltpu.VMEM((n, 8, 128), jnp.float32),
+                pltpu.SemaphoreType.DMA((2,)),
                 pltpu.SemaphoreType.DMA((n,)),
                 pltpu.SemaphoreType.DMA((n,)),
             ],
             compiler_params=pltpu.CompilerParams(collective_id=1, has_side_effects=True),
             name="giveback",
-        )(*scores)
+        )(scores)
         return pl.pallas_call(
             softmax_kernel,
             out_shape=(jax.ShapeDtypeStruct((rows, length), jnp.float32), jax.ShapeDtypeStruct((rows,), jnp.float32)),

time: 67.1 us -> 56.2 us (0.84)
  starting transfers between devices: 5.51 us -> 0 us
  local copies, waits for them, and re-layouts: 3.46 us -> 0 us
  Pallas kernels: 56.7 us -> 54.8 us
    ppermute x7 -> x0, starting transfers between devices: 5.51 us -> none  [exchange(): return lax.ppermute(x, axes, [(s, s ^ k) for s in range(n)])]
    unnamed x10 -> x0, local copies, waits for them, and re-layouts: 3.46 us -> none
    pallas_call x3 -> x1, Pallas kernels: 32.9 us -> 29.7 us  [local_step(): pl.pallas_call(score_kernel, out_shape=jax.ShapeDtypeStruct((n, 8, 128),...]
    pallas_call x1, Pallas kernels: 15.9 us -> 18.4 us  [local_step(): pl.pallas_call(functools.partial(route_kernel, shard_len, n, n_vocab), ou...]
    pallas_call x1, Pallas kernels: 6.07 us -> 4.88 us  [local_step(): pl.pallas_call(functools.partial(return_kernel, n, n_vocab), out_shape=ja...]
  transfers between devices with their start and end apart: 7 -> 0, of which waited for: 0 -> 0; matrix products, arithmetic and copies ran while one was open for 0% -> 0% of each run, Pallas kernels for 55% -> 0%
where the time goes in v6:
time: 56.2 us; the launch traced here: 55.5 us
  Pallas kernels  54.8 us (98%)
  between operations  0.65 us (1%)
    pallas_call x1, Pallas kernels, local_step(): pl.pallas_call(score_kernel, out_shape=jax.ShapeDtypeStruct((n, 8, 128),...  29.7 us
    pallas_call x1, Pallas kernels, local_step(): pl.pallas_call(functools.partial(route_kernel, shard_len, n, n_vocab), ou...  18.4 us
    pallas_call x1, Pallas kernels, local_step(): pl.pallas_call(functools.partial(return_kernel, n, n_vocab), out_shape=ja...  4.88 us
    pallas_call x1, Pallas kernels, local_step(): pl.pallas_call(softmax_kernel, out_shape=(jax.ShapeDtypeStruct((rows, len...  1.79 us

profile of v6, /device:TPU:0, one launch (start us, length us, event | category | flops | bytes accessed | tf_op | source)
XLA Modules:
  0.0 55.5 jit_solution(5416475262143152259)
XLA Ops:
  0.6 18.4 %route.1 = (s32[8,4,128]{2,1,0:T(4,128)}, s32[32,128]{1,0:T(8,128)}, bf16[8,32,5120]{2,1,0:T(8,128)(2,1)}) custom-call(s32[32,64]{1,0:T(8,128)} %ids_hbm.1, s32[32,64]{1,0:T(8,128)} %valid_hbm.1, s32[32]{0:T(128)} %tgt_hbm.1, bf16[32,5120]{1,0:T(8,128)(2,1)} %h_hbm.1), custom_call_target="tpu_custom_call" | custom-call | tf_op jit(solution)/shard_map/route/pallas_call | solution.py:298
  19.1 29.7 %score.1.sc_hbm = f32[8,8,128]{2,1,0:T(8,128)} custom-call(s32[32,128]{1,0:T(8,128)} %bitcast.6, bf16[2048,40,4,2,128]{4,3,2,1,0:T(2,128)(2,1)} %bitcast.2.w_hbm, bf16[32,8,5120]{2,1,0:T(8,128)(2,1)} %bitcast.5), custom_call_target="tpu_custom_call" | custom-call | tf_op jit(solution)/shard_map/score/pallas_call | solution.py:325
  48.8 4.9 %giveback.1.sc_ref = f32[8,8,128]{2,1,0:T(8,128)} custom-call(f32[8,8,128]{2,1,0:T(8,128)} %score.1.sc_hbm), custom_call_target="tpu_custom_call" | custom-call | tf_op jit(solution)/shard_map/giveback/pallas_call | solution.py:340
  53.7 1.8 %finish.1 = (f32[32,64]{1,0:T(8,128)}, f32[32]{0:T(128)}) custom-call(f32[8,8,128]{2,1,0:T(8,128)} %giveback.1.sc_ref, s32[32,128]{1,0:T(8,128)} %get-tuple-element.7.meta_ref), custom_call_target="tpu_custom_call" | custom-call | tf_op jit(solution)/shard_map/finish/pallas_call | solution.py:354

commit v7 on v6

--- a/solution.py
+++ b/solution.py
@@ -12,6 +12,7 @@
 CAP = 16
 SLOTS = 128
 DEPTH = 4
+WAITS = 4
 
 
 def flip_bits(a, k):
@@ -52,7 +53,7 @@
         pm, pv = peer(m, v, to, n_vocab)
         i = len(sends)
         sends.append(pltpu.make_async_remote_copy(
-            src_ref=hbuf.at[src, part], dst_ref=hbuf.at[dst, part], send_sem=hsend.at[i], recv_sem=hrecv.at[i],
+            src_ref=hbuf.at[src, part], dst_ref=(hall_out if to == 1 else hbuf).at[dst, part], send_sem=hsend.at[i], recv_sem=hrecv.at[i],
             device_id={"model": pm, "vocab": pv}, device_id_type=MESH))
         return sends[-1]
 
@@ -137,8 +138,6 @@
     y_to_x.start()
     y_p[1].start()
     keep(meta_ref, meta_out)
-    own_p.wait_recv()
-    keep(hbuf.at[1], hall_out.at[1])
     own_x[1].wait_recv()
     x_p[1].start()
     keep(hbuf.at[2], hall_out.at[2])
@@ -148,54 +147,55 @@
     for c in copies:
         c.wait_recv()
     keep(tin_ref, tbl_out)
-    for c in x_p:
-        c.wait_recv()
-    keep(hbuf.at[3], hall_out.at[3])
-    for c in y_p:
-        c.wait_recv()
-    keep(hbuf.at[5], hall_out.at[5])
     x_to_y.wait_recv()
     d_p[0].start()
     keep(hbuf.at[6, lo], hall_out.at[6, lo])
     y_to_x.wait_recv()
     d_p[1].start()
     keep(hbuf.at[6, hi], hall_out.at[6, hi])
-    d_p[0].wait_recv()
-    keep(hbuf.at[7, lo], hall_out.at[7, lo])
-    d_p[1].wait_recv()
-    keep(hbuf.at[7, hi], hall_out.at[7, hi])
+    for c in [own_p] + x_p + y_p + d_p:
+        c.wait_recv()
     for c in sends + copies:
         c.wait_send()
     for c in outs:
         c.wait()
 
 
-def score_kernel(tbl_ref, w_hbm, h_hbm, out_ref, *scratch):
+def score_kernel(tbl_hbm, w_hbm, h_hbm, out_ref, *scratch):
     bufs = scratch[:DEPTH]
-    h_ref, hf_ref, sems, hsem = scratch[DEPTH:]
+    tbl_ref, h_ref, hf_ref, sems, lsem = scratch[DEPTH:]
     tiles = w_hbm.shape[1]
     nrow = SLOTS // CAP
     quads = CAP // 4
-    chunks = tbl_ref.shape[0]
-    per = chunks // out_ref.shape[0]
+    blocks, per, _ = tbl_ref.shape
+    chunks = blocks * per
+
+    loads = [pltpu.make_async_copy(tbl_hbm.at[0], tbl_ref.at[0], lsem.at[0]),
+             pltpu.make_async_copy(tbl_hbm.at[pl.ds(1, blocks - 1)], tbl_ref.at[pl.ds(1, blocks - 1)], lsem.at[1]),
+             pltpu.make_async_copy(h_hbm, h_ref, lsem.at[2])]
+    for c in loads:
+        c.start()
 
     def issue(r, b, k):
-        at = tbl_ref[r, k]
+        at = tbl_ref[r // per, r % per, k] if isinstance(r, int) else tbl_ref[lax.div(r, per), lax.rem(r, per), k]
         t, p = lax.shift_right_logical(at, 3), lax.bitwise_and(lax.shift_right_logical(at, 1), 3)
         pltpu.make_async_copy(
-            w_hbm.at[t, :, p], bufs[b].at[k // 4, :, pl.ds(2 * (k % 4), 2), :], sems.at[b]).start(priority=k % 2)
+            w_hbm.at[t, :, p], bufs[b].at[k // 4, :, pl.ds(2 * (k % 4), 2), :], sems.at[b, k * WAITS // SLOTS]).start(priority=k % 2)
 
     lane = lax.broadcasted_iota(jnp.int32, (8, 128), 1)
 
     def work(c, b, more):
         ahead = c + DEPTH - 1
-        pltpu.make_async_copy(bufs[b], bufs[b], sems.at[b]).wait()
         flat = bufs[b].reshape(SLOTS // 4 * tiles * 8, 128)
         blk, part = lax.div(c, per), lax.rem(c, per)
         hf_ref[...] = h_ref[c].astype(jnp.float32)
         got = jnp.zeros((8, 128), jnp.float32)
         base = part * (SLOTS // 4)
         for i in range(nrow):
+            if i % (nrow // WAITS) == 0:
+                w = i // (nrow // WAITS)
+                piece = bufs[b].at[pl.ds(w * (SLOTS // 4 // WAITS), SLOTS // 4 // WAITS)]
+                pltpu.make_async_copy(piece, piece, sems.at[b, w]).wait()
             acc = [[jnp.zeros((8, 128), jnp.float32)] * 2 for _ in range(quads)]
             for kk in range(0, tiles, 2):
                 if more:
@@ -212,14 +212,12 @@
         fresh = (lane >= base) & (lane < base + SLOTS // 4)
         out_ref[blk] = jnp.where(fresh, got, out_ref[blk])
 
-    for k in range(SLOTS):
-        issue(0, 0, k)
-    hcopy = pltpu.make_async_copy(h_hbm, h_ref, hsem)
-    hcopy.start()
-    for c in range(1, DEPTH - 1):
+    loads[0].wait()
+    for c in range(DEPTH - 1):
         for k in range(SLOTS):
             issue(c, c, k)
-    hcopy.wait()
+    loads[1].wait()
+    loads[2].wait()
 
     def step(g, _):
         for b in range(DEPTH):
@@ -286,7 +284,6 @@
     vec_spec = P(("rep",) + axes)
     vmem = pl.BlockSpec(memory_space=pltpu.VMEM)
     hbm = pl.BlockSpec(memory_space=pl.ANY)
-    smem = pl.BlockSpec(memory_space=pltpu.SMEM)
 
     def local_step(hidden, head_rows, allowed_ids, valid_mask, target_pos):
         rows, length = allowed_ids.shape
@@ -325,18 +322,19 @@
         scores = pl.pallas_call(
             score_kernel,
             out_shape=jax.ShapeDtypeStruct((n, 8, 128), jnp.float32),
-            in_specs=[smem, hbm, hbm],
+            in_specs=[hbm, hbm, hbm],
             out_specs=vmem,
             scratch_shapes=[
                 *[pltpu.VMEM((SLOTS // 4, tiles, 8, 128), jnp.bfloat16)] * DEPTH,
+                pltpu.SMEM((n, per, 128), jnp.int32),
                 pltpu.VMEM((chunks, SLOTS // CAP, width), jnp.bfloat16),
                 pltpu.VMEM((SLOTS // CAP, width), jnp.float32),
-                pltpu.SemaphoreType.DMA((DEPTH,)),
-                pltpu.SemaphoreType.DMA,
+                pltpu.SemaphoreType.DMA((DEPTH, WAITS)),
+                pltpu.SemaphoreType.DMA((3,)),
             ],
             compiler_params=pltpu.CompilerParams(vmem_limit_bytes=67_000_000),
             name="score",
-        )(tbl.reshape(n * per, 128), pairs, hall.reshape(chunks, SLOTS // CAP, width))
+        )(tbl, pairs, hall.reshape(chunks, SLOTS // CAP, width))
         back = pl.pallas_call(
             functools.partial(return_kernel, n, n_vocab),
             out_shape=jax.ShapeDtypeStruct((n, 8, 128), jnp.float32),

time: 56.2 us -> 55.8 us (level)
  no operation moved by 1% of the time
where the time goes in v7:
time: 55.8 us; the launch traced here: 55.6 us
  Pallas kernels  54.9 us (98%)
  between operations  0.65 us (1%)
    pallas_call x1, Pallas kernels, local_step(): pl.pallas_call(score_kernel, out_shape=jax.ShapeDtypeStruct((n, 8, 128),...  29.9 us
    pallas_call x1, Pallas kernels, local_step(): pl.pallas_call(functools.partial(route_kernel, shard_len, n, n_vocab), ou...  18.4 us
    pallas_call x1, Pallas kernels, local_step(): pl.pallas_call(functools.partial(return_kernel, n, n_vocab), out_shape=ja...  4.82 us
    pallas_call x1, Pallas kernels, local_step(): pl.pallas_call(softmax_kernel, out_shape=(jax.ShapeDtypeStruct((rows, len...  1.79 us

profile of v7, /device:TPU:0, one launch (start us, length us, event | category | flops | bytes accessed | tf_op | source)
XLA Modules:
  0.0 55.6 jit_solution(7525369421005180848)
XLA Ops:
  0.6 18.4 %route.1 = (s32[8,4,128]{2,1,0:T(4,128)}, s32[32,128]{1,0:T(8,128)}, bf16[8,32,5120]{2,1,0:T(8,128)(2,1)}) custom-call(s32[32,64]{1,0:T(8,128)} %ids_hbm.1, s32[32,64]{1,0:T(8,128)} %valid_hbm.1, s32[32]{0:T(128)} %tgt_hbm.1, bf16[32,5120]{1,0:T(8,128)(2,1)} %h_hbm.1), custom_call_target="tpu_custom_call" | custom-call | tf_op jit(solution)/shard_map/route/pallas_call | solution.py:295
  19.0 29.9 %score.1.sc_hbm = f32[8,8,128]{2,1,0:T(8,128)} custom-call(s32[8,4,128]{2,1,0:T(4,128)} %get-tuple-element.5.tbl_hbm, bf16[2048,40,4,2,128]{4,3,2,1,0:T(2,128)(2,1)} %bitcast.1.w_hbm, bf16[32,8,5120]{2,1,0:T(8,128)(2,1)} %bitcast.4), custom_call_target="tpu_custom_call" | custom-call | tf_op jit(solution)/shard_map/score/pallas_call | solution.py:322
  48.9 4.8 %giveback.1.sc_ref = f32[8,8,128]{2,1,0:T(8,128)} custom-call(f32[8,8,128]{2,1,0:T(8,128)} %score.1.sc_hbm), custom_call_target="tpu_custom_call" | custom-call | tf_op jit(solution)/shard_map/giveback/pallas_call | solution.py:338
  53.8 1.8 %finish.1 = (f32[32,64]{1,0:T(8,128)}, f32[32]{0:T(128)}) custom-call(f32[8,8,128]{2,1,0:T(8,128)} %giveback.1.sc_ref, s32[32,128]{1,0:T(8,128)} %get-tuple-element.7.meta_ref), custom_call_target="tpu_custom_call" | custom-call | tf_op jit(solution)/shard_map/finish/pallas_call | solution.py:352

commit v8 on v7

--- a/solution.py
+++ b/solution.py
@@ -163,28 +163,28 @@
 
 def score_kernel(tbl_hbm, w_hbm, h_hbm, out_ref, *scratch):
     bufs = scratch[:DEPTH]
-    tbl_ref, h_ref, hf_ref, sems, lsem = scratch[DEPTH:]
+    tbl_ref, tbl_vmem, h_ref, hf_ref, sems, lsem = scratch[DEPTH:]
     tiles = w_hbm.shape[1]
     nrow = SLOTS // CAP
     quads = CAP // 4
     blocks, per, _ = tbl_ref.shape
     chunks = blocks * per
 
-    loads = [pltpu.make_async_copy(tbl_hbm.at[0], tbl_ref.at[0], lsem.at[0]),
-             pltpu.make_async_copy(tbl_hbm.at[pl.ds(1, blocks - 1)], tbl_ref.at[pl.ds(1, blocks - 1)], lsem.at[1]),
-             pltpu.make_async_copy(h_hbm, h_ref, lsem.at[2])]
-    for c in loads:
-        c.start()
-
-    def issue(r, b, k):
+    tload, hload = pltpu.make_async_copy(tbl_hbm, tbl_vmem, lsem.at[0]), pltpu.make_async_copy(h_hbm, h_ref, lsem.at[1])
+    tload.start()
+    hload.start()
+    first = pltpu.make_async_copy(tbl_vmem.at[0], tbl_ref.at[0], lsem.at[2])
+    rest = pltpu.make_async_copy(tbl_vmem.at[pl.ds(1, blocks - 1)], tbl_ref.at[pl.ds(1, blocks - 1)], lsem.at[3])
+
+    def issue(r, b, k, parts=1):
         at = tbl_ref[r // per, r % per, k] if isinstance(r, int) else tbl_ref[lax.div(r, per), lax.rem(r, per), k]
         t, p = lax.shift_right_logical(at, 3), lax.bitwise_and(lax.shift_right_logical(at, 1), 3)
         pltpu.make_async_copy(
-            w_hbm.at[t, :, p], bufs[b].at[k // 4, :, pl.ds(2 * (k % 4), 2), :], sems.at[b, k * WAITS // SLOTS]).start(priority=k % 2)
+            w_hbm.at[t, :, p], bufs[b].at[k // 4, :, pl.ds(2 * (k % 4), 2), :], sems.at[b, k * parts // SLOTS]).start(priority=k % 2)
 
     lane = lax.broadcasted_iota(jnp.int32, (8, 128), 1)
 
-    def work(c, b, more):
+    def work(c, b, more, parts=1, ahead_parts=1):
         ahead = c + DEPTH - 1
         flat = bufs[b].reshape(SLOTS // 4 * tiles * 8, 128)
         blk, part = lax.div(c, per), lax.rem(c, per)
@@ -192,15 +192,15 @@
         got = jnp.zeros((8, 128), jnp.float32)
         base = part * (SLOTS // 4)
         for i in range(nrow):
-            if i % (nrow // WAITS) == 0:
-                w = i // (nrow // WAITS)
-                piece = bufs[b].at[pl.ds(w * (SLOTS // 4 // WAITS), SLOTS // 4 // WAITS)]
+            if i % (nrow // parts) == 0:
+                w = i // (nrow // parts)
+                piece = bufs[b].at[pl.ds(w * (SLOTS // 4 // parts), SLOTS // 4 // parts)]
                 pltpu.make_async_copy(piece, piece, sems.at[b, w]).wait()
             acc = [[jnp.zeros((8, 128), jnp.float32)] * 2 for _ in range(quads)]
             for kk in range(0, tiles, 2):
                 if more:
                     for k in range(-(-kk * CAP // tiles), -(-(kk + 2) * CAP // tiles)):
-                        issue(ahead, (b + DEPTH - 1) % DEPTH, i * CAP + k)
+                        issue(ahead, (b + DEPTH - 1) % DEPTH, i * CAP + k, ahead_parts)
                 hb = [jnp.broadcast_to(hf_ref[i:i + 1, (kk + z) * 128:(kk + z + 1) * 128], (8, 128)) for z in (0, 1)]
                 for g in range(quads):
                     at = ((i * quads + g) * tiles + kk) * 8
@@ -212,12 +212,15 @@
         fresh = (lane >= base) & (lane < base + SLOTS // 4)
         out_ref[blk] = jnp.where(fresh, got, out_ref[blk])
 
-    loads[0].wait()
+    tload.wait()
+    first.start()
+    rest.start()
+    first.wait()
     for c in range(DEPTH - 1):
         for k in range(SLOTS):
             issue(c, c, k)
-    loads[1].wait()
-    loads[2].wait()
+    rest.wait()
+    hload.wait()
 
     def step(g, _):
         for b in range(DEPTH):
@@ -226,7 +229,7 @@
 
     lax.fori_loop(0, chunks // DEPTH - 1, step, 0)
     for b in range(DEPTH):
-        work(jnp.int32(chunks - DEPTH + b), b, b == 0)
+        work(jnp.int32(chunks - DEPTH + b), b, b == 0, WAITS if b == DEPTH - 1 else 1, WAITS)
 
 
 def return_kernel(n, n_vocab, sc_hbm, out_hbm, sc_ref, lsem, ssend, srecv):
@@ -327,10 +330,11 @@
             scratch_shapes=[
                 *[pltpu.VMEM((SLOTS // 4, tiles, 8, 128), jnp.bfloat16)] * DEPTH,
                 pltpu.SMEM((n, per, 128), jnp.int32),
+                pltpu.VMEM((n, per, 128), jnp.int32),
                 pltpu.VMEM((chunks, SLOTS // CAP, width), jnp.bfloat16),
                 pltpu.VMEM((SLOTS // CAP, width), jnp.float32),
                 pltpu.SemaphoreType.DMA((DEPTH, WAITS)),
-                pltpu.SemaphoreType.DMA((3,)),
+                pltpu.SemaphoreType.DMA((4,)),
             ],
             compiler_params=pltpu.CompilerParams(vmem_limit_bytes=67_000_000),
             name="score",

time: 55.8 us -> 55.2 us (0.989)
  Pallas kernels: 54.9 us -> 54 us
    pallas_call x1, Pallas kernels: 29.9 us -> 29 us  [local_step(): pl.pallas_call(score_kernel, out_shape=jax.ShapeDtypeStruct((n, 8, 128),...]
where the time goes in v8:
time: 55.2 us; the launch traced here: 54.6 us
  Pallas kernels  54 us (98%)
  between operations  0.65 us (1%)
    pallas_call x1, Pallas kernels, local_step(): pl.pallas_call(score_kernel, out_shape=jax.ShapeDtypeStruct((n, 8, 128),...  29 us
    pallas_call x1, Pallas kernels, local_step(): pl.pallas_call(functools.partial(route_kernel, shard_len, n, n_vocab), ou...  18.4 us
    pallas_call x1, Pallas kernels, local_step(): pl.pallas_call(functools.partial(return_kernel, n, n_vocab), out_shape=ja...  4.82 us
    pallas_call x1, Pallas kernels, local_step(): pl.pallas_call(softmax_kernel, out_shape=(jax.ShapeDtypeStruct((rows, len...  1.79 us

profile of v8, /device:TPU:0, one launch (start us, length us, event | category | flops | bytes accessed | tf_op | source)
XLA Modules:
  0.0 54.6 jit_solution(3524027775458832551)
XLA Ops:
  0.6 18.4 %route.1 = (s32[8,4,128]{2,1,0:T(4,128)}, s32[32,128]{1,0:T(8,128)}, bf16[8,32,5120]{2,1,0:T(8,128)(2,1)}) custom-call(s32[32,64]{1,0:T(8,128)} %ids_hbm.1, s32[32,64]{1,0:T(8,128)} %valid_hbm.1, s32[32]{0:T(128)} %tgt_hbm.1, bf16[32,5120]{1,0:T(8,128)(2,1)} %h_hbm.1), custom_call_target="tpu_custom_call" | custom-call | tf_op jit(solution)/shard_map/route/pallas_call | solution.py:298
  19.0 29.0 %score.1.sc_hbm = f32[8,8,128]{2,1,0:T(8,128)} custom-call(s32[8,4,128]{2,1,0:T(4,128)} %get-tuple-element.5.tbl_hbm, bf16[2048,40,4,2,128]{4,3,2,1,0:T(2,128)(2,1)} %bitcast.1.w_hbm, bf16[32,8,5120]{2,1,0:T(8,128)(2,1)} %bitcast.4), custom_call_target="tpu_custom_call" | custom-call | tf_op jit(solution)/shard_map/score/pallas_call | solution.py:325
  48.0 4.8 %giveback.1.sc_ref = f32[8,8,128]{2,1,0:T(8,128)} custom-call(f32[8,8,128]{2,1,0:T(8,128)} %score.1.sc_hbm), custom_call_target="tpu_custom_call" | custom-call | tf_op jit(solution)/shard_map/giveback/pallas_call | solution.py:342
  52.8 1.8 %finish.1 = (f32[32,64]{1,0:T(8,128)}, f32[32]{0:T(128)}) custom-call(f32[8,8,128]{2,1,0:T(8,128)} %giveback.1.sc_ref, s32[32,128]{1,0:T(8,128)} %get-tuple-element.7.meta_ref), custom_call_target="tpu_custom_call" | custom-call | tf_op jit(solution)/shard_map/finish/pallas_call | solution.py:356

commit v9 on v8

--- a/solution.py
+++ b/solution.py
@@ -171,16 +171,17 @@
     chunks = blocks * per
 
     tload, hload = pltpu.make_async_copy(tbl_hbm, tbl_vmem, lsem.at[0]), pltpu.make_async_copy(h_hbm, h_ref, lsem.at[1])
+    first = pltpu.make_async_copy(tbl_hbm.at[0], tbl_ref.at[0], lsem.at[2])
+    first.start()
     tload.start()
     hload.start()
-    first = pltpu.make_async_copy(tbl_vmem.at[0], tbl_ref.at[0], lsem.at[2])
     rest = pltpu.make_async_copy(tbl_vmem.at[pl.ds(1, blocks - 1)], tbl_ref.at[pl.ds(1, blocks - 1)], lsem.at[3])
 
     def issue(r, b, k, parts=1):
         at = tbl_ref[r // per, r % per, k] if isinstance(r, int) else tbl_ref[lax.div(r, per), lax.rem(r, per), k]
         t, p = lax.shift_right_logical(at, 3), lax.bitwise_and(lax.shift_right_logical(at, 1), 3)
         pltpu.make_async_copy(
-            w_hbm.at[t, :, p], bufs[b].at[k // 4, :, pl.ds(2 * (k % 4), 2), :], sems.at[b, k * parts // SLOTS]).start(priority=k % 2)
+            w_hbm.at[t, :, p], bufs[b].at[k // 4, :, pl.ds(2 * (k % 4), 2), :], sems.at[b, k * parts // SLOTS]).start()
 
     lane = lax.broadcasted_iota(jnp.int32, (8, 128), 1)
 
@@ -212,13 +213,12 @@
         fresh = (lane >= base) & (lane < base + SLOTS // 4)
         out_ref[blk] = jnp.where(fresh, got, out_ref[blk])
 
-    tload.wait()
-    first.start()
-    rest.start()
     first.wait()
     for c in range(DEPTH - 1):
         for k in range(SLOTS):
             issue(c, c, k)
+    tload.wait()
+    rest.start()
     rest.wait()
     hload.wait()
 

time: 55.2 us -> 54.4 us (0.986)
    pallas_call x1, Pallas kernels: 29 us -> 28.4 us  [local_step(): pl.pallas_call(score_kernel, out_shape=jax.ShapeDtypeStruct((n, 8, 128),...]
where the time goes in v9:
time: 54.4 us; the launch traced here: 54.2 us
  Pallas kernels  53.5 us (98%)
  between operations  0.65 us (1%)
    pallas_call x1, Pallas kernels, local_step(): pl.pallas_call(score_kernel, out_shape=jax.ShapeDtypeStruct((n, 8, 128),...  28.4 us
    pallas_call x1, Pallas kernels, local_step(): pl.pallas_call(functools.partial(route_kernel, shard_len, n, n_vocab), ou...  18.4 us
    pallas_call x1, Pallas kernels, local_step(): pl.pallas_call(functools.partial(return_kernel, n, n_vocab), out_shape=ja...  4.96 us
    pallas_call x1, Pallas kernels, local_step(): pl.pallas_call(softmax_kernel, out_shape=(jax.ShapeDtypeStruct((rows, len...  1.79 us

profile of v9, /device:TPU:0, one launch (start us, length us, event | category | flops | bytes accessed | tf_op | source)
XLA Modules:
  0.0 54.2 jit_solution(13626760058088422081)
XLA Ops:
  0.6 18.4 %route.1 = (s32[8,4,128]{2,1,0:T(4,128)}, s32[32,128]{1,0:T(8,128)}, bf16[8,32,5120]{2,1,0:T(8,128)(2,1)}) custom-call(s32[32,64]{1,0:T(8,128)} %ids_hbm.1, s32[32,64]{1,0:T(8,128)} %valid_hbm.1, s32[32]{0:T(128)} %tgt_hbm.1, bf16[32,5120]{1,0:T(8,128)(2,1)} %h_hbm.1), custom_call_target="tpu_custom_call" | custom-call | tf_op jit(solution)/shard_map/route/pallas_call | solution.py:298
  19.0 28.4 %score.1.sc_hbm = f32[8,8,128]{2,1,0:T(8,128)} custom-call(s32[8,4,128]{2,1,0:T(4,128)} %get-tuple-element.5.tbl_hbm, bf16[2048,40,4,2,128]{4,3,2,1,0:T(2,128)(2,1)} %bitcast.1.w_hbm, bf16[32,8,5120]{2,1,0:T(8,128)(2,1)} %bitcast.4), custom_call_target="tpu_custom_call" | custom-call | tf_op jit(solution)/shard_map/score/pallas_call | solution.py:325
  47.4 5.0 %giveback.1.sc_ref = f32[8,8,128]{2,1,0:T(8,128)} custom-call(f32[8,8,128]{2,1,0:T(8,128)} %score.1.sc_hbm), custom_call_target="tpu_custom_call" | custom-call | tf_op jit(solution)/shard_map/giveback/pallas_call | solution.py:342
  52.4 1.8 %finish.1 = (f32[32,64]{1,0:T(8,128)}, f32[32]{0:T(128)}) custom-call(f32[8,8,128]{2,1,0:T(8,128)} %giveback.1.sc_ref, s32[32,128]{1,0:T(8,128)} %get-tuple-element.7.meta_ref), custom_call_target="tpu_custom_call" | custom-call | tf_op jit(solution)/shard_map/finish/pallas_call | solution.py:356

commit v10 on v9

--- a/solution.py
+++ b/solution.py
@@ -60,10 +60,11 @@
     own_x = [send(0, 2, lo, 2), send(0, 2, hi, 2)]
     own_y = [send(0, 4, lo, 4), send(0, 4, hi, 4)]
     own_p = send(0, 1, every, 1)
-    x_to_y, y_to_x = send(2, 6, lo, 4), send(4, 6, hi, 2)
+    quarter = [pl.ds(i * half // 2, half // 2) for i in range(4)]
+    x_to_y, y_to_x = [send(2, 6, q, 4) for q in quarter[:2]], [send(4, 6, q, 2) for q in quarter[2:]]
     x_p = [send(2, 3, lo, 1), send(2, 3, hi, 1)]
     y_p = [send(4, 5, lo, 1), send(4, 5, hi, 1)]
-    d_p = [send(6, 7, lo, 1), send(6, 7, hi, 1)]
+    d_p = [send(6, 7, q, 1) for q in quarter]
 
     loads[0].wait()
     pl.semaphore_wait(barrier, n - 1)
@@ -125,17 +126,19 @@
     copies = []
     for k in range(1, n):
         pm, pv = peer(m, v, k, n_vocab)
-        c = pltpu.make_async_remote_copy(
+        copies.append(pltpu.make_async_remote_copy(
             src_ref=send_ref.at[pm * n_vocab + pv], dst_ref=tin_ref.at[k], send_sem=tsend.at[k], recv_sem=trecv.at[k],
-            device_id={"model": pm, "vocab": pv}, device_id_type=MESH)
-        c.start()
-        copies.append(c)
+            device_id={"model": pm, "vocab": pv}, device_id_type=MESH))
 
     own_x[0].wait_recv()
-    x_to_y.start()
+    for c in copies:
+        c.start()
+    for c in x_to_y:
+        c.start()
     x_p[0].start()
     own_y[1].wait_recv()
-    y_to_x.start()
+    for c in y_to_x:
+        c.start()
     y_p[1].start()
     keep(meta_ref, meta_out)
     own_x[1].wait_recv()
@@ -147,12 +150,12 @@
     for c in copies:
         c.wait_recv()
     keep(tin_ref, tbl_out)
-    x_to_y.wait_recv()
-    d_p[0].start()
-    keep(hbuf.at[6, lo], hall_out.at[6, lo])
-    y_to_x.wait_recv()
-    d_p[1].start()
-    keep(hbuf.at[6, hi], hall_out.at[6, hi])
+    for i in range(2):
+        x_to_y[i].wait_recv()
+        d_p[i].start()
+        y_to_x[i].wait_recv()
+        d_p[2 + i].start()
+    keep(hbuf.at[6], hall_out.at[6])
     for c in [own_p] + x_p + y_p + d_p:
         c.wait_recv()
     for c in sends + copies:
@@ -313,8 +316,8 @@
                 pltpu.VMEM((n, rows, width), jnp.bfloat16),
                 pltpu.SemaphoreType.DMA((n,)),
                 pltpu.SemaphoreType.DMA((n,)),
-                pltpu.SemaphoreType.DMA((13,)),
-                pltpu.SemaphoreType.DMA((13,)),
+                pltpu.SemaphoreType.DMA((17,)),
+                pltpu.SemaphoreType.DMA((17,)),
                 pltpu.SemaphoreType.DMA((4,)),
                 pltpu.SemaphoreType.DMA((12,)),
             ],

time: 54.4 us -> 54.5 us (level)
  no operation moved by 1% of the time
where the time goes in v10:
time: 54.5 us; the launch traced here: 54.1 us
  Pallas kernels  53.5 us (98%)
  between operations  0.65 us (1%)
    pallas_call x1, Pallas kernels, local_step(): pl.pallas_call(score_kernel, out_shape=jax.ShapeDtypeStruct((n, 8, 128),...  28.6 us
    pallas_call x1, Pallas kernels, local_step(): pl.pallas_call(functools.partial(route_kernel, shard_len, n, n_vocab), ou...  18.2 us
    pallas_call x1, Pallas kernels, local_step(): pl.pallas_call(functools.partial(return_kernel, n, n_vocab), out_shape=ja...  4.91 us
    pallas_call x1, Pallas kernels, local_step(): pl.pallas_call(softmax_kernel, out_shape=(jax.ShapeDtypeStruct((rows, len...  1.79 us

profile of v10, /device:TPU:0, one launch (start us, length us, event | category | flops | bytes accessed | tf_op | source)
XLA Modules:
  0.0 54.1 jit_solution(13792799633059554228)
XLA Ops:
  0.6 18.2 %route.1 = (s32[8,4,128]{2,1,0:T(4,128)}, s32[32,128]{1,0:T(8,128)}, bf16[8,32,5120]{2,1,0:T(8,128)(2,1)}) custom-call(s32[32,64]{1,0:T(8,128)} %ids_hbm.1, s32[32,64]{1,0:T(8,128)} %valid_hbm.1, s32[32]{0:T(128)} %tgt_hbm.1, bf16[32,5120]{1,0:T(8,128)(2,1)} %h_hbm.1), custom_call_target="tpu_custom_call" | custom-call | tf_op jit(solution)/shard_map/route/pallas_call | solution.py:301
  18.8 28.6 %score.1.sc_hbm = f32[8,8,128]{2,1,0:T(8,128)} custom-call(s32[8,4,128]{2,1,0:T(4,128)} %get-tuple-element.5.tbl_hbm, bf16[2048,40,4,2,128]{4,3,2,1,0:T(2,128)(2,1)} %bitcast.1.w_hbm, bf16[32,8,5120]{2,1,0:T(8,128)(2,1)} %bitcast.4), custom_call_target="tpu_custom_call" | custom-call | tf_op jit(solution)/shard_map/score/pallas_call | solution.py:328
  47.4 4.9 %giveback.1.sc_ref = f32[8,8,128]{2,1,0:T(8,128)} custom-call(f32[8,8,128]{2,1,0:T(8,128)} %score.1.sc_hbm), custom_call_target="tpu_custom_call" | custom-call | tf_op jit(solution)/shard_map/giveback/pallas_call | solution.py:345
  52.3 1.8 %finish.1 = (f32[32,64]{1,0:T(8,128)}, f32[32]{0:T(128)}) custom-call(f32[8,8,128]{2,1,0:T(8,128)} %giveback.1.sc_ref, s32[32,128]{1,0:T(8,128)} %get-tuple-element.7.meta_ref), custom_call_target="tpu_custom_call" | custom-call | tf_op jit(solution)/shard_map/finish/pallas_call | solution.py:359

commit v11 on v10

--- a/solution.py
+++ b/solution.py
@@ -26,20 +26,22 @@
     return flip_bits(m, k // n_vocab), flip_bits(v, k % n_vocab)
 
 
-def entry_barrier(n, n_vocab, m, v):
-    barrier = pltpu.get_barrier_semaphore()
-    for k in range(1, n):
+def signal_peers(sem, ks, n_vocab, m, v):
+    for k in ks:
         pm, pv = peer(m, v, k, n_vocab)
-        pl.semaphore_signal(barrier, inc=1, device_id={"model": pm, "vocab": pv}, device_id_type=MESH)
-    return barrier
+        pl.semaphore_signal(sem, inc=1, device_id={"model": pm, "vocab": pv}, device_id_type=MESH)
+
+
+NEAR = (1, 2, 4)
 
 
 def route_kernel(shard_len, n, n_vocab, ids_hbm, valid_hbm, tgt_hbm, h_hbm, tbl_out, meta_out, hall_out,
-                 ids_ref, valid_ref, tgt_ref, meta_ref, t_ref, send_ref, tin_ref, hbuf, tsend, trecv, hsend, hrecv, lsem, osem):
+                 ids_ref, valid_ref, tgt_ref, meta_ref, t_ref, send_ref, tin_ref, hbuf, tsend, trecv, hsend, hrecv, lsem, osem, round_sem):
     rows, length = ids_ref.shape
     m, v = lax.axis_index("model"), lax.axis_index("vocab")
     me = m * n_vocab + v
-    barrier = entry_barrier(n, n_vocab, m, v)
+    barrier = pltpu.get_barrier_semaphore()
+    signal_peers(barrier, NEAR, n_vocab, m, v)
     loads = [pltpu.make_async_copy(src, dst, lsem.at[i]) for i, (src, dst) in enumerate(
         ((h_hbm, hbuf.at[0]), (ids_hbm, ids_ref), (valid_hbm, valid_ref), (tgt_hbm, tgt_ref)))]
     for c in loads:
@@ -67,9 +69,10 @@
     d_p = [send(6, 7, q, 1) for q in quarter]
 
     loads[0].wait()
-    pl.semaphore_wait(barrier, n - 1)
+    pl.semaphore_wait(barrier, len(NEAR))
     for c in (own_x[0], own_y[1], own_p, own_x[1], own_y[0]):
         c.start()
+    signal_peers(round_sem.at[0], NEAR, n_vocab, m, v)
     outs = []
 
     def keep(src, dst):
@@ -130,7 +133,10 @@
             src_ref=send_ref.at[pm * n_vocab + pv], dst_ref=tin_ref.at[k], send_sem=tsend.at[k], recv_sem=trecv.at[k],
             device_id={"model": pm, "vocab": pv}, device_id_type=MESH))
 
+    pl.semaphore_wait(round_sem.at[0], len(NEAR))
+    signal_peers(round_sem.at[1], NEAR, n_vocab, m, v)
     own_x[0].wait_recv()
+    pl.semaphore_wait(round_sem.at[1], len(NEAR))
     for c in copies:
         c.start()
     for c in x_to_y:
@@ -238,7 +244,8 @@
 def return_kernel(n, n_vocab, sc_hbm, out_hbm, sc_ref, lsem, ssend, srecv):
     m, v = lax.axis_index("model"), lax.axis_index("vocab")
     me = m * n_vocab + v
-    barrier = entry_barrier(n, n_vocab, m, v)
+    barrier = pltpu.get_barrier_semaphore()
+    signal_peers(barrier, range(1, n), n_vocab, m, v)
     load = pltpu.make_async_copy(sc_hbm, sc_ref, lsem.at[0])
     load.start()
     load.wait()
@@ -320,6 +327,7 @@
                 pltpu.SemaphoreType.DMA((17,)),
                 pltpu.SemaphoreType.DMA((4,)),
                 pltpu.SemaphoreType.DMA((12,)),
+                pltpu.SemaphoreType.REGULAR((2,)),
             ],
             compiler_params=pltpu.CompilerParams(collective_id=0, has_side_effects=True),
             name="route",

time: 54.5 us -> 53.8 us (0.987)
  Pallas kernels: 53.5 us -> 52.7 us
    pallas_call x1, Pallas kernels: 18.2 us -> 17.7 us  [local_step(): pl.pallas_call(functools.partial(route_kernel, shard_len, n, n_vocab), ou...]
where the time goes in v11:
time: 53.8 us; the launch traced here: 53.4 us
  Pallas kernels  52.7 us (98%)
  between operations  0.65 us (1%)
    pallas_call x1, Pallas kernels, local_step(): pl.pallas_call(score_kernel, out_shape=jax.ShapeDtypeStruct((n, 8, 128),...  28.5 us
    pallas_call x1, Pallas kernels, local_step(): pl.pallas_call(functools.partial(route_kernel, shard_len, n, n_vocab), ou...  17.7 us
    pallas_call x1, Pallas kernels, local_step(): pl.pallas_call(functools.partial(return_kernel, n, n_vocab), out_shape=ja...  4.82 us
    pallas_call x1, Pallas kernels, local_step(): pl.pallas_call(softmax_kernel, out_shape=(jax.ShapeDtypeStruct((rows, len...  1.79 us

profile of v11, /device:TPU:0, one launch (start us, length us, event | category | flops | bytes accessed | tf_op | source)
XLA Modules:
  0.0 53.4 jit_solution(11174692439010199358)
XLA Ops:
  0.6 17.7 %route.1 = (s32[8,4,128]{2,1,0:T(4,128)}, s32[32,128]{1,0:T(8,128)}, bf16[8,32,5120]{2,1,0:T(8,128)(2,1)}) custom-call(s32[32,64]{1,0:T(8,128)} %ids_hbm.1, s32[32,64]{1,0:T(8,128)} %valid_hbm.1, s32[32]{0:T(128)} %tgt_hbm.1, bf16[32,5120]{1,0:T(8,128)(2,1)} %h_hbm.1), custom_call_target="tpu_custom_call" | custom-call | tf_op jit(solution)/shard_map/route/pallas_call | solution.py:308
  18.3 28.5 %score.1.sc_hbm = f32[8,8,128]{2,1,0:T(8,128)} custom-call(s32[8,4,128]{2,1,0:T(4,128)} %get-tuple-element.5.tbl_hbm, bf16[2048,40,4,2,128]{4,3,2,1,0:T(2,128)(2,1)} %bitcast.1.w_hbm, bf16[32,8,5120]{2,1,0:T(8,128)(2,1)} %bitcast.4), custom_call_target="tpu_custom_call" | custom-call | tf_op jit(solution)/shard_map/score/pallas_call | solution.py:336
  46.8 4.8 %giveback.1.sc_ref = f32[8,8,128]{2,1,0:T(8,128)} custom-call(f32[8,8,128]{2,1,0:T(8,128)} %score.1.sc_hbm), custom_call_target="tpu_custom_call" | custom-call | tf_op jit(solution)/shard_map/giveback/pallas_call | solution.py:353
  51.6 1.8 %finish.1 = (f32[32,64]{1,0:T(8,128)}, f32[32]{0:T(128)}) custom-call(f32[8,8,128]{2,1,0:T(8,128)} %giveback.1.sc_ref, s32[32,128]{1,0:T(8,128)} %get-tuple-element.7.meta_ref), custom_call_target="tpu_custom_call" | custom-call | tf_op jit(solution)/shard_map/finish/pallas_call | solution.py:367

commit v12 on v11

--- a/solution.py
+++ b/solution.py
@@ -42,13 +42,14 @@
     me = m * n_vocab + v
     barrier = pltpu.get_barrier_semaphore()
     signal_peers(barrier, NEAR, n_vocab, m, v)
-    loads = [pltpu.make_async_copy(src, dst, lsem.at[i]) for i, (src, dst) in enumerate(
-        ((h_hbm, hbuf.at[0]), (ids_hbm, ids_ref), (valid_hbm, valid_ref), (tgt_hbm, tgt_ref)))]
-    for c in loads:
-        c.start()
-
     half = rows // 2
     lo, hi, every = pl.ds(0, half), pl.ds(half, half), pl.ds(0, rows)
+    loads = [pltpu.make_async_copy(src, dst, lsem.at[i]) for i, (src, dst) in enumerate(
+        ((h_hbm.at[lo], hbuf.at[0, lo]), (h_hbm.at[hi], hbuf.at[0, hi]), (ids_hbm, ids_ref), (valid_hbm, valid_ref),
+         (tgt_hbm, tgt_ref)))]
+    for c in loads:
+        c.start()
+
     sends = []
 
     def send(src, dst, part, to):
@@ -68,9 +69,11 @@
     y_p = [send(4, 5, lo, 1), send(4, 5, hi, 1)]
     d_p = [send(6, 7, q, 1) for q in quarter]
 
+    pl.semaphore_wait(barrier, len(NEAR))
     loads[0].wait()
-    pl.semaphore_wait(barrier, len(NEAR))
-    for c in (own_x[0], own_y[1], own_p, own_x[1], own_y[0]):
+    own_x[0].start()
+    loads[1].wait()
+    for c in (own_y[1], own_p, own_x[1], own_y[0]):
         c.start()
     signal_peers(round_sem.at[0], NEAR, n_vocab, m, v)
     outs = []
@@ -80,7 +83,7 @@
         outs[-1].start()
 
     keep(hbuf.at[0], hall_out.at[0])
-    for c in loads[1:]:
+    for c in loads[2:]:
         c.wait()
 
     ids = ids_ref[...]
@@ -251,7 +254,7 @@
     load.wait()
     pl.semaphore_wait(barrier, n - 1)
     copies = []
-    for k in range(1, n):
+    for k in reversed(range(1, n)):
         pm, pv = peer(m, v, k, n_vocab)
         c = pltpu.make_async_remote_copy(
             src_ref=sc_ref.at[k], dst_ref=out_hbm.at[me], send_sem=ssend.at[k], recv_sem=srecv.at[k],
@@ -325,7 +328,7 @@
                 pltpu.SemaphoreType.DMA((n,)),
                 pltpu.SemaphoreType.DMA((17,)),
                 pltpu.SemaphoreType.DMA((17,)),
-                pltpu.SemaphoreType.DMA((4,)),
+                pltpu.SemaphoreType.DMA((5,)),
                 pltpu.SemaphoreType.DMA((12,)),
                 pltpu.SemaphoreType.REGULAR((2,)),
             ],

time: 53.8 us -> 53.9 us (level)
  no operation moved by 1% of the time
where the time goes in v12:
time: 53.9 us; the launch traced here: 53.8 us
  Pallas kernels  53.2 us (99%)
  between operations  0.65 us (1%)
    pallas_call x1, Pallas kernels, local_step(): pl.pallas_call(score_kernel, out_shape=jax.ShapeDtypeStruct((n, 8, 128),...  28.9 us
    pallas_call x1, Pallas kernels, local_step(): pl.pallas_call(functools.partial(route_kernel, shard_len, n, n_vocab), ou...  17.7 us
    pallas_call x1, Pallas kernels, local_step(): pl.pallas_call(functools.partial(return_kernel, n, n_vocab), out_shape=ja...  4.78 us
    pallas_call x1, Pallas kernels, local_step(): pl.pallas_call(softmax_kernel, out_shape=(jax.ShapeDtypeStruct((rows, len...  1.79 us

profile of v12, /device:TPU:0, one launch (start us, length us, event | category | flops | bytes accessed | tf_op | source)
XLA Modules:
  0.0 53.8 jit_solution(5263464831441032281)
XLA Ops:
  0.6 17.7 %route.1 = (s32[8,4,128]{2,1,0:T(4,128)}, s32[32,128]{1,0:T(8,128)}, bf16[8,32,5120]{2,1,0:T(8,128)(2,1)}) custom-call(s32[32,64]{1,0:T(8,128)} %ids_hbm.1, s32[32,64]{1,0:T(8,128)} %valid_hbm.1, s32[32]{0:T(128)} %tgt_hbm.1, bf16[32,5120]{1,0:T(8,128)(2,1)} %h_hbm.1), custom_call_target="tpu_custom_call" | custom-call | tf_op jit(solution)/shard_map/route/pallas_call | solution.py:311
  18.3 28.9 %score.1.sc_hbm = f32[8,8,128]{2,1,0:T(8,128)} custom-call(s32[8,4,128]{2,1,0:T(4,128)} %get-tuple-element.5.tbl_hbm, bf16[2048,40,4,2,128]{4,3,2,1,0:T(2,128)(2,1)} %bitcast.1.w_hbm, bf16[32,8,5120]{2,1,0:T(8,128)(2,1)} %bitcast.4), custom_call_target="tpu_custom_call" | custom-call | tf_op jit(solution)/shard_map/score/pallas_call | solution.py:339
  47.3 4.8 %giveback.1.sc_ref = f32[8,8,128]{2,1,0:T(8,128)} custom-call(f32[8,8,128]{2,1,0:T(8,128)} %score.1.sc_hbm), custom_call_target="tpu_custom_call" | custom-call | tf_op jit(solution)/shard_map/giveback/pallas_call | solution.py:356
  52.0 1.8 %finish.1 = (f32[32,64]{1,0:T(8,128)}, f32[32]{0:T(128)}) custom-call(f32[8,8,128]{2,1,0:T(8,128)} %giveback.1.sc_ref, s32[32,128]{1,0:T(8,128)} %get-tuple-element.7.meta_ref), custom_call_target="tpu_custom_call" | custom-call | tf_op jit(solution)/shard_map/finish/pallas_call | solution.py:370
